TPU v7x, 32 devices: a whole 2x2x4 slice. The times are simulated.
32 devices in a mesh: band: 8 (over z, y), sub: 4 (over x, core).
Axes of the slice: x: 2, y: 2, z: 4, core: 2. Of those that a mesh axis runs over, the one named last changes fastest.
Arguments:
- grid_x: bfloat16 [227, 16384], P(None, ('band', 'sub')), may hold values from -6 to 6
- mesh_in: bfloat16 [2048, 512], P(('band', 'sub')), may hold values from -6 to 6
- w_embed: bfloat16 [227, 512], replicated, may hold values from -0.375 to 0.375
- w_src: bfloat16 [512, 512], replicated, may hold values from -0.25 to 0.25
- w_dst: bfloat16 [512, 512], replicated, may hold values from -0.25 to 0.25
- w_edge: bfloat16 [512, 512], replicated, may hold values from -0.25 to 0.25
- w_proc: bfloat16 [512, 512], replicated, may hold values from -0.25 to 0.25
- w_recv: bfloat16 [512, 512], replicated, may hold values from -0.25 to 0.25
- g2m_src: int32 [2048, 40], P(('band', 'sub')), may hold values from 0 to 16383, as said below
- mesh_src: int32 [2048, 6], P(('band', 'sub')), may hold values from 0 to 2047, as said below
- cotangent: bfloat16 [2048, 512], P(('band', 'sub')), may hold values from -6 to 6
Outputs:
- mesh_out: bfloat16 [2048, 512], P(('band', 'sub'))
- grid_grad: float32 [227, 16384], P(None, ('band', 'sub'))
- src_grad: float32 [512, 512], replicated
- edge_grad: float32 [512, 512], replicated
Inputs may be any that keep to these rules, and one draw needn't show every extreme that they name: Grid node g belongs to band g // (512 * 4), mesh node m to band m // (64 * 4); g2m_src[m, k] lies in the band of mesh node m, or among the 512 grid nodes of an adjacent band that stand next to that band in index order. mesh_src[m, j] lies in the band of mesh node m, or among the 64 mesh nodes of an adjacent band that stand next to that band in index order.
All inputs are finite; a program needn't handle non-finite values.
Results may differ from a plain program's by a relative error of at most 0.015.
Values may be sent and summed in bfloat16 or wider, within the bound.
A program may use at most 128 MiB of HBM per device.

v0:
```python
import math

import jax
import jax.numpy as jnp
from jax import lax
from jax.sharding import PartitionSpec as P

EPSILON = 1e-05


def padded(shard, sides, width):
    for axis, dim in sides:
        devices, length = (lax.axis_size(axis), shard.shape[dim])
        up = [(i, (i + 1) % devices) for i in range(devices - 1)]
        down = [(j, i) for i, j in up]
        last = lax.slice_in_dim(shard, length - width, length, axis=dim)
        first = lax.slice_in_dim(shard, 0, width, axis=dim)
        before = lax.ppermute(last, axis, up)
        after = lax.ppermute(first, axis, down)
        shard = jnp.concatenate([before, shard, after], axis=dim)
    return shard


def from_behind(value, axis, steps):
    count = lax.axis_size(axis)
    first, last = (max(0, -steps), min(count, count - steps))
    return lax.ppermute(value, axis, [(source, source + steps) for source in range(first, last)])


def silu_slope(value):
    sigma = jax.nn.sigmoid(value)
    return sigma * (1.0 + value * (1.0 - sigma))


def normalize(value):
    centred = value - jnp.mean(value, axis=-1, keepdims=True)
    spread = jnp.sqrt(jnp.mean(centred * centred, axis=-1, keepdims=True) + EPSILON)
    return (centred / spread, spread)


def times_transpose(left, right):
    return lax.dot_general(
        left, right, (((1,), (1,)), ((), ())), preferred_element_type=jnp.float32
    )


def first_contract(left, right):
    return lax.dot_general(
        left, right, (((0,), (0,)), ((), ())), preferred_element_type=jnp.float32
    )


def fetch_grid(projected):
    border = projected.shape[0]
    block = lax.all_gather(projected, "sub", axis=0, tiled=True)
    return padded(block, (("band", 0),), border)


def return_grid(window_grad, border):
    middle = window_grad[border:-border]
    from_above = from_behind(window_grad[:border].astype(jnp.bfloat16), "band", -1).astype(
        jnp.float32
    )
    from_below = from_behind(window_grad[-border:].astype(jnp.bfloat16), "band", 1).astype(
        jnp.float32
    )
    middle = middle.at[:border].add(from_below)
    middle = middle.at[middle.shape[0] - border :].add(from_above)
    return lax.psum_scatter(
        middle.astype(jnp.bfloat16), "sub", scatter_dimension=0, tiled=True
    ).astype(jnp.float32)


def return_mesh(window_grad, border):
    middle = window_grad[border:-border]
    from_above = from_behind(window_grad[:border].astype(jnp.bfloat16), "band", -1).astype(
        jnp.float32
    )
    from_below = from_behind(window_grad[-border:].astype(jnp.bfloat16), "band", 1).astype(
        jnp.float32
    )
    middle = middle.at[:border].add(from_below)
    middle = middle.at[middle.shape[0] - border :].add(from_above)
    return lax.psum_scatter(
        middle.astype(jnp.bfloat16), "sub", scatter_dimension=0, tiled=True
    ).astype(jnp.float32)


def body(
    grid_x, mesh_in, w_embed, w_src, w_dst, w_edge, w_proc, w_recv, g2m_src, mesh_src, cotangent
):
    latent = w_src.shape[0]
    mesh_rows, enc_count = g2m_src.shape
    mesh_count = mesh_src.shape[1]
    band_index = lax.axis_index("band")
    groups = lax.axis_size("sub")
    hidden_pre = first_contract(grid_x, w_embed)
    hidden_grid = jax.nn.silu(hidden_pre).astype(jnp.bfloat16)
    projected = jnp.dot(hidden_grid, w_src, preferred_element_type=jnp.float32).astype(jnp.bfloat16)
    dest_term = jnp.dot(mesh_in, w_dst, preferred_element_type=jnp.float32)
    grid_border = projected.shape[0]
    grid_window = fetch_grid(projected)
    grid_base = band_index * (grid_border * groups) - grid_border
    grid_local = (g2m_src - grid_base).reshape(-1)
    before = jnp.take(grid_window, grid_local, axis=0).astype(jnp.float32)
    before = (before.reshape(mesh_rows, enc_count, latent) + dest_term[:, None, :]).reshape(
        -1, latent
    )
    active = jax.nn.silu(before).astype(jnp.bfloat16)
    normed, spread = normalize(jnp.dot(active, w_edge, preferred_element_type=jnp.float32))
    encoded = jnp.sum(normed.reshape(mesh_rows, enc_count, latent), axis=1)
    hidden_mesh = (mesh_in.astype(jnp.float32) + encoded / math.sqrt(enc_count)).astype(
        jnp.bfloat16
    )
    query = jnp.dot(hidden_mesh, w_proc, preferred_element_type=jnp.float32).astype(jnp.bfloat16)
    receiver = jnp.dot(hidden_mesh, w_recv, preferred_element_type=jnp.float32)
    mesh_border = query.shape[0]
    mesh_block = lax.all_gather(query, "sub", axis=0, tiled=True)
    mesh_window = padded(mesh_block, (("band", 0),), mesh_border)
    mesh_base = band_index * mesh_block.shape[0] - mesh_border
    mesh_local = (mesh_src - mesh_base).reshape(-1)
    mesh_before = jnp.take(mesh_window, mesh_local, axis=0).astype(jnp.float32)
    mesh_before = mesh_before.reshape(mesh_rows, mesh_count, latent) + receiver[:, None, :]
    summed = jnp.sum(jax.nn.silu(mesh_before), axis=1)
    mesh_out = (hidden_mesh.astype(jnp.float32) + summed / math.sqrt(mesh_count)).astype(
        jnp.bfloat16
    )
    upstream = cotangent.astype(jnp.float32)
    mesh_slope = (upstream / math.sqrt(mesh_count))[:, None, :] * silu_slope(mesh_before)
    receiver_grad = jnp.sum(mesh_slope, axis=1)
    window_grad = jnp.zeros((mesh_window.shape[0], latent), jnp.float32)
    window_grad = window_grad.at[mesh_local].add(mesh_slope.reshape(-1, latent))
    query_grad = return_mesh(window_grad, mesh_border)
    mesh_grad = upstream + times_transpose(query_grad.astype(jnp.bfloat16), w_proc)
    mesh_grad = mesh_grad + times_transpose(receiver_grad.astype(jnp.bfloat16), w_recv)
    upper = mesh_grad / math.sqrt(enc_count)
    incoming = jnp.broadcast_to(upper[:, None, :], (mesh_rows, enc_count, latent)).reshape(
        -1, latent
    )
    centred_grad = incoming - jnp.mean(incoming, axis=-1, keepdims=True)
    centred_grad = centred_grad - normed * jnp.mean(incoming * normed, axis=-1, keepdims=True)
    norm_grad = (centred_grad / spread).astype(jnp.bfloat16)
    edge_part = first_contract(active, norm_grad)
    before_grad = times_transpose(norm_grad, w_edge) * silu_slope(before)
    grid_window_grad = (
        jnp.zeros((grid_window.shape[0], latent), jnp.float32).at[grid_local].add(before_grad)
    )
    projected_grad = return_grid(grid_window_grad, grid_border)
    projected_low = projected_grad.astype(jnp.bfloat16)
    src_part = first_contract(hidden_grid, projected_low)
    hidden_grad = (times_transpose(projected_low, w_src) * silu_slope(hidden_pre)).astype(
        jnp.bfloat16
    )
    grid_grad = times_transpose(w_embed, hidden_grad)
    src_grad, edge_grad = lax.psum((src_part, edge_part), ("band", "sub"))
    return (mesh_out, grid_grad, src_grad, edge_grad)


def solution(mesh):
    placed = (
        P(None, ("band", "sub")),
        P(("band", "sub"), None),
        P(),
        P(),
        P(),
        P(),
        P(),
        P(),
        P(("band", "sub"), None),
        P(("band", "sub"), None),
        P(("band", "sub"), None),
    )
    return jax.shard_map(
        body,
        mesh=mesh,
        in_specs=placed,
        out_specs=(P(("band", "sub"), None), P(None, ("band", "sub")), P(), P()),
        check_vma=False,
    )
```

profile of v0, /device:TPU:13, one launch (start us, length us, event | category | flops | bytes accessed | tf_op | source)
XLA Modules:
  0.0 405.5 jit_solution(17956858091147088192)
XLA Ops:
  7.3 1.4 fusion.53
  9.7 2.4 convolution_convert_fusion
  15.9 20.4 %all-gather.2.cloned.1.call-done = bf16[2048,512]{1,0:T(8,128)(2,1)} async-done(((bf16[512,512]{1,0:T(8,128)(2,1)}), bf16[2048,512]{1,0:T(8,128)(2,1)}) %all-gather.2.cloned.1.call-update) | async-done | bytes 2097168 | tf_op jit(solution)/shard_map/all_gather | solution.py:55
  36.3 1.3 fusion.48
  37.6 3.1 collective-permute-start
  40.7 2.2 collective-permute-start.1
  43.1 20.8 %collective-permute-done = bf16[512,512]{1,0:T(8,128)(2,1)S(1)} collective-permute-done((bf16[512,512]{1,0:T(8,128)(2,1)S(1)}, bf16[512,512]{1,0:T(8,128)(2,1)S(1)}, u32[]{:S(2)}, u32[]{:S(2)}) %collective-permute-start) | collective-permute-done | bytes 524320 | tf_op jit(solution)/shard_map/ppermute | solution.py:18
  63.9 3.0 pad_maximum_fusion
  66.9 10.6 %gather_fusion = bf16[2560,512]{1,0:T(8,128)(2,1)} fusion(bf16[3072,512]{1,0:T(8,128)(2,1)} %pad_maximum_fusion, s32[3072]{0:T(1024)S(1)} %pad_clamp_fusion), kind=kCustom, calls=%fused_computation | custom fusion | bytes 5253120 | tf_op jit(solution)/shard_map/jit(_take)/gather | solution.py:105
  77.5 5.7 %bitcast_add_fusion = (f32[2560,512]{1,0:T(8,128)}, bf16[2560,512]{1,0:T(8,128)(2,1)S(1)}) fusion(f32[64,512]{1,0:T(8,128)S(1)} %fusion.54, bf16[2560,512]{1,0:T(8,128)(2,1)} %gather_fusion, pred[2560]{0:T(1024)(128)(4,1)S(1)} %compare_and_fusion), kind=kLoop, calls=%fused_computation.10 | loop fusion | flops 10485760 | bytes 10619392 | tf_op jit(solution)/shard_map/add | solution.py:106
  83.2 1.6 fusion.51
  85.8 3.4 subtract_divide_fusion
  89.2 3.4 reduce_sum.67
  92.6 1.3 convolution_convert_fusion.1
  93.9 6.8 %all_gather.7 = bf16[256,512]{1,0:T(8,128)(2,1)S(1)} all-gather(bf16[64,512]{1,0:T(8,128)(2,1)S(1)} %convolution_convert_fusion.1), channel_id=1, replica_groups=mesh['band'=8,'sub'=4] {'sub'}, dimensions={0}, use_global_device_ids=true | all-gather | bytes 327680 | tf_op jit(solution)/shard_map/all_gather | solution.py:118
  101.4 4.0 collective-permute-start.2
  105.4 2.1 collective-permute-start.3
  107.5 1.2 fusion.55
  109.4 1.1 add.186
  110.5 2.2 add.192
  113.4 1.0 pad_maximum_fusion.1
  114.4 2.6 gather_fusion.1
  117.0 5.1 %scatter_custom_fusion = f32[384,512]{1,0:T(8,128)} fusion(s32[384]{0:T(512)} %copy-done.23, f32[384,512]{1,0:T(8,128)} %mul.82, f32[384,512]{1,0:T(8,128)} %add.192, bf16[384,512]{1,0:T(8,128)(2,1)} %gather_fusion.1, f32[]{:T(128)} %constant.173.clone.1, f32[]{:T(128)} %constant.175.clone.1, pred[384]{0:T(512)(128)(4,1)} %compare_and_fusion.2, ...), kind=kCustom, calls=%fused_computation.47 | custom fusion | flops 2359296 | bytes 2754560 | tf_op jit(solution)/shard_map/scatter-add | solution.py:132
  122.1 1.2 convert.8
  123.3 4.3 %collective-permute-start.4 = (bf16[64,512]{1,0:T(8,128)(2,1)S(1)}, bf16[64,512]{1,0:T(8,128)(2,1)S(1)}, u32[]{:S(2)}, u32[]{:S(2)}) collective-permute-start(bf16[64,512]{1,0:T(8,128)(2,1)S(1)} %get-tuple-element.65), channel_id=1, source_target_pairs={{0,4},{4,8},{8,12},{12,16},{16,20},{20,24},{24,28},{1,5},{5,9},{9,... | collective-permute-start | bytes 196616 | tf_op jit(solution)/shard_map/ppermute | solution.py:27
  127.5 1.1 slice.134
  128.6 1.9 collective-permute-start.5
  131.5 3.0 collective-permute-done.5
  137.0 2.9 multiply_reduce_fusion.1
  140.0 15.9 %reduce-scatter.3.cloned.1.call-done = bf16[64,512]{1,0:T(8,128)(2,1)} async-done(((bf16[256,512]{1,0:T(8,128)(2,1)}), bf16[64,512]{1,0:T(8,128)(2,1)}) %reduce-scatter.3.cloned.1.call-update) | async-done | bytes 65552 | tf_op jit(solution)/shard_map/reduce_scatter | solution.py:84
  155.9 1.3 convolution_add_fusion.1
  157.2 1.4 fusion.52
  158.7 3.6 fusion.3
  162.5 3.9 fusion.2
  166.4 3.9 fusion.56
  170.4 21.5 %scatter_custom_fusion.1 = f32[3072,512]{1,0:T(8,128)} fusion(s32[2560]{0:T(1024)} %copy-done.21, f32[2560,512]{1,0:T(8,128)} %fusion.56, f32[2560,512]{1,0:T(8,128)} %get-tuple-element.60, f32[]{:T(128)} %constant.175.clone.1, f32[]{:T(128)} %constant.173.clone.1), kind=kCustom, calls=%fused_computation.11 | custom fusion | flops 11796480 | bytes 16778240 | tf_op jit(solution)/shard_map/scatter-add | solution.py:146
  191.9 3.2 convert.9
  195.2 3.5 collective-permute-start.6
  198.7 2.2 collective-permute-start.7
  200.9 20.6 %collective-permute-done.6 = bf16[512,512]{1,0:T(8,128)(2,1)S(1)} collective-permute-done((bf16[512,512]{1,0:T(8,128)(2,1)S(1)}, bf16[512,512]{1,0:T(8,128)(2,1)S(1)}, u32[]{:S(2)}, u32[]{:S(2)}) %collective-permute-start.6) | collective-permute-done | bytes 524320 | tf_op jit(solution)/shard_map/ppermute | solution.py:27
  221.9 1.6 convert_element_type.93
  223.6 4.2 %fusion.57 = f32[512,512]{1,0:T(8,128)} fusion(bf16[2560,512]{1,0:T(8,128)(2,1)S(1)} %get-tuple-element.61, bf16[2560,512]{1,0:T(8,128)(2,1)} %copy-done.3), kind=kOutput, calls=%fused_computation.105 | convolution fusion | flops 1342177280 | bytes 6291456 | tf_op jit(solution)/shard_map/dot_general | solution.py:48
  227.9 27.6 %reduce-scatter.5.cloned.1.call-done = bf16[512,512]{1,0:T(8,128)(2,1)} async-done(((bf16[2048,512]{1,0:T(8,128)(2,1)}), bf16[512,512]{1,0:T(8,128)(2,1)}) %reduce-scatter.5.cloned.1.call-update) | async-done | bytes 524304 | tf_op jit(solution)/shard_map/reduce_scatter | solution.py:69
  255.4 2.9 fusion.46
  259.0 1.7 fusion.14
  260.7 133.8 %all-reduce.3.cloned.1.call-done = (f32[512,512]{1,0:T(8,128)}, f32[512,512]{1,0:T(8,128)}) async-done(((f32[512,512]{1,0:T(8,128)}, f32[512,512]{1,0:T(8,128)}), (f32[512,512]{1,0:T(8,128)}, f32[512,512]{1,0:T(8,128)})) %all-reduce.3.cloned.1.call-update) | async-done | bytes 2097168 | tf_op jit(solution)/shard_map/psum | solution.py:155
  394.5 2.3 copy.27
  396.7 2.3 copy.28
  (108 shorter events, 12.8 us)
Async XLA Ops:
  7.2 76.0 %copy-start = (bf16[512,512]{1,0:T(8,128)(2,1)S(1)}, bf16[512,512]{1,0:T(8,128)(2,1)}, u32[]{:S(2)}) copy-start(bf16[512,512]{1,0:T(8,128)(2,1)} %param.24) | copy-start | bytes 1572868
  7.2 4.9 %copy-start.22 = (s32[64,40]{0,1:T(8,128)S(1)}, s32[64,40]{0,1:T(8,128)}, u32[]{:S(2)}) copy-start(s32[64,40]{0,1:T(8,128)} %param.27) | copy-start | bytes 30724
  7.2 5.2 %copy-start.25 = (s32[64,6]{0,1:T(8,128)S(1)}, s32[64,6]{0,1:T(8,128)}, u32[]{:S(2)}) copy-start(s32[64,6]{0,1:T(8,128)} %param.28) | copy-start | bytes 4612
  7.2 6.2 %copy-start.14 = (bf16[64,512]{1,0:T(8,128)(2,1)S(1)}, bf16[64,512]{1,0:T(8,128)(2,1)}, u32[]{:S(2)}) copy-start(bf16[64,512]{1,0:T(8,128)(2,1)} %param.29) | copy-start | bytes 196612
  7.2 29.1 %all-gather.2.cloned.1.call-start = ((), (), s32[]{:S(2)}) async-start(), calls=%async_computation.2 | async-start | bytes 2621440 | tf_op jit(solution)/shard_map/all_gather | solution.py:55
  8.7 1.0 copy-start.8
  9.7 33.2 %copy-start.13 = (bf16[512,512]{1,0:T(8,128)(2,1)S(1)}, bf16[512,512]{1,0:T(8,128)(2,1)}, u32[]{:S(2)}) copy-start(bf16[512,512]{1,0:T(8,128)(2,1)} %param.23) | copy-start | bytes 1572868
  9.7 33.2 %copy-start.15 = (bf16[64,512]{1,0:T(8,128)(2,1)S(1)}, bf16[64,512]{1,0:T(8,128)(2,1)}, u32[]{:S(2)}) copy-start(bf16[64,512]{1,0:T(8,128)(2,1)} %param.20) | copy-start | bytes 196612
  12.1 143.8 %reduce-scatter.3.cloned.1.call-start = ((), (), s32[]{:S(2)}) async-start(), calls=%async_computation.3 | async-start | bytes 327680 | tf_op jit(solution)/shard_map/reduce_scatter | solution.py:84
  13.4 0.7 copy-start.6
  15.2 51.6 %copy-start.21 = (s32[2560]{0:T(1024)}, s32[2560]{0:T(1024)S(1)}, u32[]{:S(2)}) copy-start(s32[2560]{0:T(1024)S(1)} %fusion.43) | copy-start | bytes 30724
  15.3 27.6 %copy-start.23 = (s32[384]{0:T(512)}, s32[384]{0:T(512)S(1)}, u32[]{:S(2)}) copy-start(s32[384]{0:T(512)S(1)} %fusion.44) | copy-start | bytes 4612
  37.6 26.3 %collective-permute-start = (bf16[512,512]{1,0:T(8,128)(2,1)S(1)}, bf16[512,512]{1,0:T(8,128)(2,1)S(1)}, u32[]{:S(2)}, u32[]{:S(2)}) collective-permute-start(bf16[512,512]{1,0:T(8,128)(2,1)S(1)} %get-tuple-element.62), channel_id=1, source_target_pairs={{0,4},{4,8},{8,12},{12,16},{16,20},{20,24},{24,28},{1,5},{5,9},{9,... | collective-permute-start | bytes 1572872 | tf_op jit(solution)/shard_map/ppermute | solution.py:18
  40.7 23.2 %collective-permute-start.1 = (bf16[512,512]{1,0:T(8,128)(2,1)S(1)}, bf16[512,512]{1,0:T(8,128)(2,1)S(1)}, u32[]{:S(2)}, u32[]{:S(2)}) collective-permute-start(bf16[512,512]{1,0:T(8,128)(2,1)S(1)} %get-tuple-element.63), channel_id=1, source_target_pairs={{4,0},{8,4},{12,8},{16,12},{20,16},{24,20},{28,24},{5,1},{9,5},{13... | collective-permute-start | bytes 1572872 | tf_op jit(solution)/shard_map/ppermute | solution.py:19
  84.8 4.4 %copy-start.1 = (f32[2560,512]{1,0:T(8,128)}, f32[2560,512]{1,0:T(8,128)S(1)}, u32[]{:S(2)}) copy-start(f32[2560,512]{1,0:T(8,128)S(1)} %get-tuple-element.69) | copy-start | bytes 15728644
  85.7 3.5 copy-start.18
  89.2 3.4 copy-start.16
  92.6 14.9 %copy-start.10 = (bf16[64,512]{1,0:T(8,128)(2,1)}, bf16[64,512]{1,0:T(8,128)(2,1)S(1)}, u32[]{:S(2)}) copy-start(bf16[64,512]{1,0:T(8,128)(2,1)S(1)} %add_convert_fusion.1) | copy-start | bytes 196612
  100.7 0.7 copy-start.5
  101.4 11.4 %collective-permute-start.2 = (bf16[64,512]{1,0:T(8,128)(2,1)S(1)}, bf16[64,512]{1,0:T(8,128)(2,1)S(1)}, u32[]{:S(2)}, u32[]{:S(2)}) collective-permute-start(bf16[64,512]{1,0:T(8,128)(2,1)S(1)} %get-tuple-element.66), channel_id=1, source_target_pairs={{0,4},{4,8},{8,12},{12,16},{16,20},{20,24},{24,28},{1,5},{5,9},{9,... | collective-permute-start | bytes 196616 | tf_op jit(solution)/shard_map/ppermute | solution.py:18
  105.4 8.0 %collective-permute-start.3 = (bf16[64,512]{1,0:T(8,128)(2,1)S(1)}, bf16[64,512]{1,0:T(8,128)(2,1)}, u32[]{:S(2)}, u32[]{:S(2)}) collective-permute-start(bf16[64,512]{1,0:T(8,128)(2,1)S(1)} %get-tuple-element.67), channel_id=1, source_target_pairs={{4,0},{8,4},{12,8},{16,12},{20,16},{24,20},{28,24},{5,1},{9,5},{13... | collective-permute-start | bytes 196616 | tf_op jit(solution)/shard_map/ppermute | solution.py:19
  108.8 0.6 copy-start.7
  112.8 0.6 copy-start.20
  117.0 18.4 %copy-start.24 = (pred[64,6]{0,1:T(8,128)(4,1)S(1)}, pred[64,6]{0,1:T(8,128)(4,1)}, u32[]{:S(2)}) copy-start(pred[64,6]{0,1:T(8,128)(4,1)} %get-tuple-element.56) | copy-start | bytes 1156
  117.0 19.1 %copy-start.4 = (bf16[384,512]{1,0:T(8,128)(2,1)S(1)}, bf16[384,512]{1,0:T(8,128)(2,1)}, u32[]{:S(2)}) copy-start(bf16[384,512]{1,0:T(8,128)(2,1)} %gather_fusion.1) | copy-start | bytes 1179652
  123.3 7.3 %collective-permute-start.4 = (bf16[64,512]{1,0:T(8,128)(2,1)S(1)}, bf16[64,512]{1,0:T(8,128)(2,1)S(1)}, u32[]{:S(2)}, u32[]{:S(2)}) collective-permute-start(bf16[64,512]{1,0:T(8,128)(2,1)S(1)} %get-tuple-element.65), channel_id=1, source_target_pairs={{0,4},{4,8},{8,12},{12,16},{16,20},{20,24},{24,28},{1,5},{5,9},{9,... | collective-permute-start | bytes 196616 | tf_op jit(solution)/shard_map/ppermute | solution.py:27
  128.6 5.9 %collective-permute-start.5 = (bf16[64,512]{1,0:T(8,128)(2,1)S(1)}, bf16[64,512]{1,0:T(8,128)(2,1)S(1)}, u32[]{:S(2)}, u32[]{:S(2)}) collective-permute-start(bf16[64,512]{1,0:T(8,128)(2,1)S(1)} %get-tuple-element.64), channel_id=1, source_target_pairs={{4,0},{8,4},{12,8},{16,12},{20,16},{24,20},{28,24},{5,1},{9,5},{13... | collective-permute-start | bytes 196616 | tf_op jit(solution)/shard_map/ppermute | solution.py:27
  135.4 120.1 %reduce-scatter.5.cloned.1.call-start = ((), (), s32[]{:S(2)}) async-start(), calls=%async_computation.4 | async-start | bytes 2621440 | tf_op jit(solution)/shard_map/reduce_scatter | solution.py:69
  137.0 25.4 %copy-start.19 = (f32[2560]{0:T(1024)S(1)}, f32[2560]{0:T(1024)}, u32[]{:S(2)}) copy-start(f32[2560]{0:T(1024)} %copy-done.18) | copy-start | bytes 30724
  166.4 4.0 copy-start.3
  195.1 26.3 %copy-start.2 = (f32[3072,512]{1,0:T(8,128)S(1)}, f32[3072,512]{1,0:T(8,128)}, u32[]{:S(2)}) copy-start(f32[3072,512]{1,0:T(8,128)} %scatter_custom_fusion.1) | copy-start | bytes 18874372
  195.1 26.3 %slice-start = ((f32[3072,512]{1,0:T(8,128)}), f32[2048,512]{1,0:T(8,128)S(1)}, s32[]{:S(2)}) async-start(f32[3072,512]{1,0:T(8,128)} %scatter_custom_fusion.1), calls=%async_computation.6 | async-start | bytes 8388608 | tf_op jit(solution)/shard_map/slice | solution.py:60
  195.2 26.2 %collective-permute-start.6 = (bf16[512,512]{1,0:T(8,128)(2,1)S(1)}, bf16[512,512]{1,0:T(8,128)(2,1)S(1)}, u32[]{:S(2)}, u32[]{:S(2)}) collective-permute-start(bf16[512,512]{1,0:T(8,128)(2,1)S(1)} %get-tuple-element.59), channel_id=1, source_target_pairs={{0,4},{4,8},{8,12},{12,16},{16,20},{20,24},{24,28},{1,5},{5,9},{9,... | collective-permute-start | bytes 1572872 | tf_op jit(solution)/shard_map/ppermute | solution.py:27
  198.7 22.9 %collective-permute-start.7 = (bf16[512,512]{1,0:T(8,128)(2,1)S(1)}, bf16[512,512]{1,0:T(8,128)(2,1)S(1)}, u32[]{:S(2)}, u32[]{:S(2)}) collective-permute-start(bf16[512,512]{1,0:T(8,128)(2,1)S(1)} %get-tuple-element.58), channel_id=1, source_target_pairs={{4,0},{8,4},{12,8},{16,12},{20,16},{24,20},{28,24},{5,1},{9,5},{13... | collective-permute-start | bytes 1572872 | tf_op jit(solution)/shard_map/ppermute | solution.py:27
  223.5 170.9 %all-reduce.3.cloned.1.call-start = ((), (), s32[]{:S(2)}) async-start(), calls=%async_computation.5 | async-start | bytes 4194304 | tf_op jit(solution)/shard_map/psum | solution.py:155
  227.8 30.5 %copy-start.11 = (bf16[64,512]{1,0:T(8,128)(2,1)S(1)}, bf16[64,512]{1,0:T(8,128)(2,1)}, u32[]{:S(2)}) copy-start(bf16[64,512]{1,0:T(8,128)(2,1)} %copy-done.10) | copy-start | bytes 196612
  227.8 30.5 %copy-start.12 = (f32[64,512]{1,0:T(8,128)S(1)}, f32[64,512]{1,0:T(8,128)}, u32[]{:S(2)}) copy-start(f32[64,512]{1,0:T(8,128)} %get-tuple-element.53) | copy-start | bytes 393220
  227.8 31.2 %copy-start.9 = (f32[512,512]{1,0:T(8,128)S(1)}, f32[512,512]{1,0:T(8,128)}, u32[]{:S(2)}) copy-start(f32[512,512]{1,0:T(8,128)} %copy-done.8) | copy-start | bytes 3145732
  227.8 31.2 %copy-start.17 = (bf16[227,512]{1,0:T(8,128)(2,1)S(1)}, bf16[227,512]{1,0:T(8,128)(2,1)}, u32[]{:S(2)}) copy-start(bf16[227,512]{1,0:T(8,128)(2,1)} %param.21) | copy-start | bytes 697348
  227.9 31.2 %copy-start.26 = (bf16[512,512]{1,0:T(8,128)(2,1)S(1)}, bf16[512,512]{1,0:T(8,128)(2,1)}, u32[]{:S(2)}) copy-start(bf16[512,512]{1,0:T(8,128)(2,1)} %param.22) | copy-start | bytes 1572868
  255.4 3.6 copy-start.27
Sparse Core Ops, SparseCore 0:
  12.2 24.0 all-gather.1
  135.5 20.3 reduce-scatter.2
  223.7 31.7 reduce-scatter.4
  261.4 133.0 all-reduce.2
where the time goes:
time: 410 us; the launch traced here: 406 us
  waiting for transfers between devices  242 us (59%)
  other arithmetic  64.6 us (16%)
  local copies, waits for them, and re-layouts  30.7 us (7%)
  matrix products  23.6 us (6%)
  starting transfers between devices  23.4 us (6%)
  between operations  14.3 us (3%)
  blocking collectives  6.76 us (2%)
    psum x1, waiting for transfers between devices, body(): src_grad, edge_grad = lax.psum((src_part, edge_part), ('band', 'sub'))  134 us
    reduce_scatter x1, waiting for transfers between devices, return_grid(): lax.psum_scatter(middle.astype(jnp.bfloat16), 'sub', scatter_dimension=0,...  27.6 us
    ppermute x4, waiting for transfers between devices, from_behind(): lax.ppermute(value, axis, [(source, source + steps) for source in range(f...  23.6 us
    scatter-add x1, other arithmetic, body(): jnp.zeros((grid_window.shape[0], latent), jnp.float32).at[grid_local]  21.5 us
    ppermute x2, waiting for transfers between devices, padded(): before = lax.ppermute(last, axis, up)  20.8 us
    all_gather x1, waiting for transfers between devices, fetch_grid(): block = lax.all_gather(projected, 'sub', axis=0, tiled=True)  20.4 us
    reduce_scatter x1, waiting for transfers between devices, return_mesh(): lax.psum_scatter(middle.astype(jnp.bfloat16), 'sub', scatter_dimension=0,...  15.9 us
    ppermute x4, starting transfers between devices, from_behind(): lax.ppermute(value, axis, [(source, source + steps) for source in range(f...  11.9 us
  transfers between devices with their start and end apart: 12, of which 7 were waited for; matrix products, arithmetic and copies ran while one was open for 5% of the time, Pallas kernels for 0%

commit v1 on v0

v1 whole, which is shorter than its diff:
```python
import functools
import math

import jax
import jax.numpy as jnp
from jax import lax
from jax.experimental import pallas as pl
from jax.experimental.pallas import tpu as pltpu
from jax.sharding import PartitionSpec as P

EPSILON = 1e-05
F32 = jnp.float32
BF16 = jnp.bfloat16
VMEM = pl.BlockSpec(memory_space=pltpu.VMEM)


def silu_slope(value):
    sigma = jax.nn.sigmoid(value)
    return sigma * (1.0 + value * (1.0 - sigma))


def normalize(value):
    centred = value - jnp.mean(value, axis=-1, keepdims=True)
    spread = jnp.sqrt(jnp.mean(centred * centred, axis=-1, keepdims=True) + EPSILON)
    return (centred / spread, spread)


def times_transpose(left, right):
    return lax.dot_general(left, right, (((1,), (1,)), ((), ())), preferred_element_type=F32)


def first_contract(left, right):
    return lax.dot_general(left, right, (((0,), (0,)), ((), ())), preferred_element_type=F32)


def remote(src, dst, send, recv, device):
    return pltpu.make_async_remote_copy(
        src_ref=src,
        dst_ref=dst,
        send_sem=send,
        recv_sem=recv,
        device_id=device,
        device_id_type=pl.DeviceIdType.MESH,
    )


def greet(barrier, device):
    pl.semaphore_signal(barrier, inc=1, device_id=device, device_id_type=pl.DeviceIdType.MESH)


def near_barrier(bands, subs, band, me):
    barrier = pltpu.get_barrier_semaphore()
    for step in range(1, subs):
        greet(barrier, (band, lax.rem(me + step, subs)))

    @pl.when(band > 0)
    def _():
        for other in range(subs):
            greet(barrier, (band - 1, other))

    @pl.when(band < bands - 1)
    def _():
        for other in range(subs):
            greet(barrier, (band + 1, other))

    sides = jnp.minimum(band, 1) + jnp.minimum(bands - 1 - band, 1)
    pl.semaphore_wait(barrier, subs - 1 + subs * sides)


def place(subs):
    band, me = (lax.axis_index("band"), lax.axis_index("sub"))
    core = lax.rem(me, 2)
    return (band, me, core, me // 2, me + 1 - 2 * core, subs // 2)


def window_kernel(bands, subs, x_ref, o_ref, send, recv, local):
    band, me, core, chip, partner, chips = place(subs)
    near_barrier(bands, subs, band, me)
    own = pltpu.make_async_copy(x_ref, o_ref.at[1 + me], local)
    own.start()

    def push(src, slot, b, s, index):
        return remote(src, o_ref.at[slot], send.at[index], recv.at[slot], (b, s))

    def arrived(slot):
        push(x_ref, slot, band, partner, 0).wait_recv()

    across = [
        push(x_ref, 1 + me, band, 2 * lax.rem(chip + k, chips) + core, k - 1)
        for k in range(1, chips)
    ]
    pair = push(x_ref, 1 + me, band, partner, chips - 1)
    rising = (me == subs - 1) & (band < bands - 1)
    falling = (me == 0) & (band > 0)

    def up(k):
        return push(x_ref, 0, band + 1, 2 * k + 1, chips + k)

    def down(k):
        return push(x_ref, subs + 1, band - 1, 2 * k, 2 * chips + k)

    @pl.when(rising)
    def _():
        for k in range(chips):
            up(k).start()

    @pl.when(falling)
    def _():
        for k in range(chips):
            down(k).start()

    for copy in across:
        copy.start()
    pair.start()
    relays = []
    for k in range(1, chips):
        source = lax.rem(chip + chips - k, chips)
        slot = 1 + 2 * source + core
        arrived(slot)
        relay = push(o_ref.at[slot], slot, band, partner, 3 * chips + k - 1)
        relay.start()
        relays.append(relay)

    below = (core == 1) & (band > 0)
    above = (core == 0) & (band < bands - 1)
    relay_below = push(o_ref.at[0], 0, band, partner, 4 * chips - 1)
    relay_above = push(o_ref.at[subs + 1], subs + 1, band, partner, 4 * chips)

    @pl.when(below)
    def _():
        arrived(0)
        relay_below.start()

    @pl.when(above)
    def _():
        arrived(subs + 1)
        relay_above.start()

    @pl.when(band == 0)
    def _():
        o_ref[0] = jnp.zeros(o_ref.shape[1:], o_ref.dtype)

    @pl.when(band == bands - 1)
    def _():
        o_ref[subs + 1] = jnp.zeros(o_ref.shape[1:], o_ref.dtype)

    arrived(1 + partner)
    for k in range(1, chips):
        source = lax.rem(chip + chips - k, chips)
        arrived(2 + 2 * source - core)

    @pl.when((core == 0) & (band > 0))
    def _():
        arrived(0)

    @pl.when((core == 1) & (band < bands - 1))
    def _():
        arrived(subs + 1)

    for copy in across + [pair] + relays:
        copy.wait_send()

    @pl.when(rising)
    def _():
        for k in range(chips):
            up(k).wait_send()

    @pl.when(falling)
    def _():
        for k in range(chips):
            down(k).wait_send()

    @pl.when(below)
    def _():
        relay_below.wait_send()

    @pl.when(above)
    def _():
        relay_above.wait_send()

    own.wait()


def fetch_window(block, bands, subs, ident):
    chips = subs // 2
    return pl.pallas_call(
        functools.partial(window_kernel, bands, subs),
        out_shape=jax.ShapeDtypeStruct((subs + 2,) + block.shape, block.dtype),
        in_specs=[VMEM],
        out_specs=VMEM,
        scratch_shapes=[
            pltpu.SemaphoreType.DMA((4 * chips + 1,)),
            pltpu.SemaphoreType.DMA((subs + 2,)),
            pltpu.SemaphoreType.DMA,
        ],
        compiler_params=pltpu.CompilerParams(collective_id=ident, has_side_effects=True),
        name=f"window{ident}",
    )(block)


def return_kernel(
    bands, subs, g_ref, o_ref, pairbuf, stage, far, edge, send1, recv1, send2, far_sem, edge_sem
):
    band, me, core, chip, partner, chips = place(subs)
    near_barrier(bands, subs, band, me)
    order = list(range(1, chips)) + [chips, 0]

    def slot_of(step, which):
        if step == chips:
            return (1 - which) * (subs + 1)
        return 1 + 2 * lax.rem(chip + step, chips) + which

    swaps = {}
    for step in order:
        swaps[step] = remote(
            g_ref.at[slot_of(step, 1 - core)],
            pairbuf.at[step],
            send1.at[step],
            recv1.at[step],
            (band, partner),
        )
        swaps[step].start()

    def combined(step):
        swaps[step].wait_recv()
        return g_ref[slot_of(step, core)].astype(F32) + pairbuf[step].astype(F32)

    across = []
    for step in range(1, chips):
        stage[step - 1] = combined(step).astype(BF16)
        copy = remote(
            stage.at[step - 1],
            far.at[step - 1],
            send2.at[step - 1],
            far_sem.at[step - 1],
            (band, 2 * lax.rem(chip + step, chips) + core),
        )
        copy.start()
        across.append(copy)
    stage[chips - 1] = combined(chips).astype(BF16)

    def border(b, s):
        return remote(
            stage.at[chips - 1], edge.at[chip], send2.at[chips - 1], edge_sem.at[chip], (b, s)
        )

    below = (core == 1) & (band > 0)
    above = (core == 0) & (band < bands - 1)

    @pl.when(below)
    def _():
        border(band - 1, subs - 1).start()

    @pl.when(above)
    def _():
        border(band + 1, 0).start()

    total = combined(0)
    for step, copy in enumerate(across):
        copy.wait_recv()
        total = total + far[step].astype(F32)
    o_ref[...] = total

    def add_edges():
        extra = o_ref[...]
        for k in range(chips):
            remote(
                stage.at[chips - 1], edge.at[k], send2.at[chips - 1], edge_sem.at[k], (band, partner)
            ).wait_recv()
            extra = extra + edge[k].astype(F32)
        o_ref[...] = extra

    @pl.when((me == subs - 1) & (band < bands - 1))
    def _():
        add_edges()

    @pl.when((me == 0) & (band > 0))
    def _():
        add_edges()

    for step in order:
        swaps[step].wait_send()
    for copy in across:
        copy.wait_send()

    @pl.when(below)
    def _():
        border(band - 1, subs - 1).wait_send()

    @pl.when(above)
    def _():
        border(band + 1, 0).wait_send()


def return_window(slots, bands, subs, ident):
    chips = subs // 2
    block = slots.shape[1:]
    return pl.pallas_call(
        functools.partial(return_kernel, bands, subs),
        out_shape=jax.ShapeDtypeStruct(block, F32),
        in_specs=[VMEM],
        out_specs=VMEM,
        scratch_shapes=[
            pltpu.VMEM((chips + 1,) + block, BF16),
            pltpu.VMEM((chips,) + block, BF16),
            pltpu.VMEM((chips,) + block, BF16),
            pltpu.VMEM((chips,) + block, BF16),
            pltpu.SemaphoreType.DMA((chips + 1,)),
            pltpu.SemaphoreType.DMA((chips + 1,)),
            pltpu.SemaphoreType.DMA((chips,)),
            pltpu.SemaphoreType.DMA((chips,)),
            pltpu.SemaphoreType.DMA((chips,)),
        ],
        compiler_params=pltpu.CompilerParams(collective_id=ident, has_side_effects=True),
        name=f"return{ident}",
    )(slots)


def sum_kernel(
    bands, subs, v_ref, o_ref, r1, a1, r2, a2, r3, s1, q1, s2, q2, s3, q3, s4, q4, s5, q5, s6, q6
):
    band, me, core, chip, partner, chips = place(subs)
    barrier = pltpu.get_barrier_semaphore()
    greet(barrier, (band, partner))
    for k in range(1, chips):
        greet(barrier, (band, 2 * lax.rem(chip + k, chips) + core))
    for i in range(1, bands):
        greet(barrier, (lax.rem(band + i, bands), me))
    pl.semaphore_wait(barrier, chips + bands - 1)
    half = chips * bands

    def part(which, step):
        return pl.ds(which * half + lax.rem(chip + step, chips) * bands, bands)

    order = list(range(1, chips)) + [0]
    swaps = {}
    for step in order:
        swaps[step] = remote(
            v_ref.at[part(1 - core, step)], r1.at[step], s1.at[step], q1.at[step], (band, partner)
        )
        swaps[step].start()
    waits = list(swaps.values())
    across = []
    for step in order:
        swaps[step].wait_recv()
        total = v_ref[part(core, step)].astype(F32) + r1[step].astype(F32)
        if step > 0:
            a1[step] = total.astype(BF16)
            copy = remote(
                a1.at[step],
                r2.at[step],
                s2.at[step],
                q2.at[step],
                (band, 2 * lax.rem(chip + step, chips) + core),
            )
            copy.start()
            across.append(copy)
    for step, copy in enumerate(across):
        copy.wait_recv()
        total = total + r2[step + 1].astype(F32)
    waits += across
    a2[...] = total.astype(BF16)
    spread = []
    for i in range(1, bands):
        goal = lax.rem(band + i, bands)
        copy = remote(a2.at[goal], r3.at[i], s3.at[i], q3.at[i], (goal, me))
        copy.start()
        spread.append(copy)
    total = a2[band].astype(F32)
    for i, copy in enumerate(spread):
        copy.wait_recv()
        total = total + r3[i + 1].astype(F32)
    waits += spread
    mine = core * half + chip * bands + band
    o_ref[mine] = total.astype(BF16)
    spread = []
    for i in range(1, bands):
        copy = remote(
            o_ref.at[mine], o_ref.at[mine], s4.at[i], q4.at[i], (lax.rem(band + i, bands), me)
        )
        copy.start()
        spread.append(copy)
    for copy in spread:
        copy.wait_recv()
    waits += spread
    across = []
    for step in range(1, chips):
        copy = remote(
            o_ref.at[part(core, 0)],
            o_ref.at[part(core, 0)],
            s5.at[step],
            q5.at[step],
            (band, 2 * lax.rem(chip + step, chips) + core),
        )
        copy.start()
        across.append(copy)
    relays = [
        remote(
            o_ref.at[part(core, 0)], o_ref.at[part(core, 0)], s6.at[0], q6.at[0], (band, partner)
        )
    ]
    relays[0].start()
    for step, copy in enumerate(across):
        copy.wait_recv()
        rows = part(core, chips - step - 1)
        relay = remote(
            o_ref.at[rows], o_ref.at[rows], s6.at[step + 1], q6.at[step + 1], (band, partner)
        )
        relay.start()
        relays.append(relay)
    for relay in relays:
        relay.wait_recv()
    for copy in waits + across + relays:
        copy.wait_send()


def sum_all(value, bands, subs, ident):
    chips = subs // 2
    count = bands * subs
    rows, latent = value.shape
    deep = rows // count
    value = value.reshape(count, deep, latent)
    dma = pltpu.SemaphoreType.DMA
    total = pl.pallas_call(
        functools.partial(sum_kernel, bands, subs),
        out_shape=jax.ShapeDtypeStruct(value.shape, BF16),
        in_specs=[VMEM],
        out_specs=VMEM,
        scratch_shapes=[
            pltpu.VMEM((chips, bands, deep, latent), BF16),
            pltpu.VMEM((chips, bands, deep, latent), BF16),
            pltpu.VMEM((chips, bands, deep, latent), BF16),
            pltpu.VMEM((bands, deep, latent), BF16),
            pltpu.VMEM((bands, deep, latent), BF16),
        ]
        + [dma((chips,)), dma((chips,))] * 2
        + [dma((bands,)), dma((bands,))] * 2
        + [dma((chips,)), dma((chips,))] * 2,
        compiler_params=pltpu.CompilerParams(collective_id=ident, has_side_effects=True),
        name=f"sum{ident}",
    )(value)
    return total.reshape(rows, latent)


def one_hot(index, count):
    return (index[:, None] == lax.broadcasted_iota(jnp.int32, (1, count), 1)).astype(BF16)


def body(
    bands, subs,
    grid_x, mesh_in, w_embed, w_src, w_dst, w_edge, w_proc, w_recv, g2m_src, mesh_src, cotangent
):
    latent = w_src.shape[0]
    channels, nodes = grid_x.shape
    mesh_rows, enc_count = g2m_src.shape
    mesh_count = mesh_src.shape[1]
    slots = subs + 2
    band_index = lax.axis_index("band")

    x_window = fetch_window(grid_x, bands, subs, 0)
    hidden_pre = lax.dot_general(
        x_window, w_embed, (((1,), (0,)), ((), ())), preferred_element_type=F32
    ).reshape(slots * nodes, latent)
    hidden = jax.nn.silu(hidden_pre).astype(BF16)
    projected = jnp.dot(hidden, w_src, preferred_element_type=F32).astype(BF16)
    dest_term = jnp.dot(mesh_in, w_dst, preferred_element_type=F32)
    grid_local = (g2m_src - (band_index * (nodes * subs) - nodes)).reshape(-1)
    before = jnp.take(projected, grid_local, axis=0).astype(F32)
    before = (before.reshape(mesh_rows, enc_count, latent) + dest_term[:, None, :]).reshape(
        -1, latent
    )
    active = jax.nn.silu(before).astype(BF16)
    normed, spread = normalize(jnp.dot(active, w_edge, preferred_element_type=F32))
    encoded = jnp.sum(normed.reshape(mesh_rows, enc_count, latent), axis=1)
    hidden_mesh = (mesh_in.astype(F32) + encoded / math.sqrt(enc_count)).astype(BF16)
    query = jnp.dot(hidden_mesh, w_proc, preferred_element_type=F32).astype(BF16)
    receiver = jnp.dot(hidden_mesh, w_recv, preferred_element_type=F32)
    mesh_window = fetch_window(query, bands, subs, 1).reshape(slots * mesh_rows, latent)
    mesh_local = (mesh_src - (band_index * (mesh_rows * subs) - mesh_rows)).T.reshape(-1)
    picks = one_hot(mesh_local, slots * mesh_rows)
    mesh_before = jnp.dot(picks, mesh_window, preferred_element_type=F32)
    mesh_before = mesh_before.reshape(mesh_count, mesh_rows, latent) + receiver[None]
    summed = jnp.sum(jax.nn.silu(mesh_before), axis=0)
    mesh_out = (hidden_mesh.astype(F32) + summed / math.sqrt(mesh_count)).astype(BF16)
    upstream = cotangent.astype(F32)
    mesh_slope = (upstream / math.sqrt(mesh_count))[None] * silu_slope(mesh_before)
    receiver_grad = jnp.sum(mesh_slope, axis=0)
    query_window = first_contract(picks, mesh_slope.reshape(-1, latent).astype(BF16)).astype(BF16)
    query_grad = return_window(query_window.reshape(slots, mesh_rows, latent), bands, subs, 2)
    mesh_grad = upstream + times_transpose(query_grad.astype(BF16), w_proc)
    mesh_grad = mesh_grad + times_transpose(receiver_grad.astype(BF16), w_recv)
    upper = mesh_grad / math.sqrt(enc_count)
    incoming = jnp.broadcast_to(upper[:, None, :], (mesh_rows, enc_count, latent)).reshape(
        -1, latent
    )
    centred_grad = incoming - jnp.mean(incoming, axis=-1, keepdims=True)
    centred_grad = centred_grad - normed * jnp.mean(incoming * normed, axis=-1, keepdims=True)
    norm_grad = (centred_grad / spread).astype(BF16)
    edge_part = first_contract(active, norm_grad)
    before_grad = (times_transpose(norm_grad, w_edge) * silu_slope(before)).astype(BF16)
    window_grad = first_contract(one_hot(grid_local, slots * nodes), before_grad).astype(BF16)
    src_part = first_contract(hidden, window_grad)
    hidden_grad = (times_transpose(window_grad, w_src) * silu_slope(hidden_pre)).astype(BF16)
    grid_part = lax.dot_general(
        w_embed,
        hidden_grad.reshape(slots, nodes, latent),
        (((1,), (2,)), ((), ())),
        preferred_element_type=F32,
    )
    grid_part = jnp.swapaxes(grid_part, 0, 1).astype(BF16)
    grid_grad = return_window(grid_part, bands, subs, 3)
    parts = jnp.concatenate([src_part, edge_part], axis=0).astype(BF16)
    sums = sum_all(parts, bands, subs, 4).astype(F32)
    return (mesh_out, grid_grad, sums[:latent], sums[latent:])


def solution(mesh):
    nodes = P(("band", "sub"), None)
    placed = (P(None, ("band", "sub")), nodes) + (P(),) * 6 + (nodes,) * 3
    return jax.shard_map(
        functools.partial(body, mesh.shape["band"], mesh.shape["sub"]),
        mesh=mesh,
        in_specs=placed,
        out_specs=(nodes, P(None, ("band", "sub")), P(), P()),
        check_vma=False,
    )
```

time: 410 us -> 173 us (0.42)
  waiting for transfers between devices: 242 us -> 0 us
  Pallas kernels: 0 us -> 85.7 us
  other arithmetic: 64.6 us -> 22 us
  starting transfers between devices: 23.4 us -> 0 us
  matrix products: 23.6 us -> 45.5 us
  between operations: 14.3 us -> 1.05 us
  local copies, waits for them, and re-layouts: 30.7 us -> 17.6 us
  blocking collectives: 6.76 us -> 0 us
    psum x1 -> x0, waiting for transfers between devices: 134 us -> none  [body(): src_grad, edge_grad = lax.psum((src_part, edge_part), ('band', 'sub'))]
    pallas_call x0 -> x5, Pallas kernels: none -> 85.7 us  [the longest x1 36.6 us: sum_all(): pl.pallas_call(functools.partial(sum_kernel, bands, subs), out_shape=jax....]
    ppermute x8 -> x0, waiting for transfers between devices: 44.4 us -> none  [the longest x4 23.6 us: from_behind(): lax.ppermute(value, axis, [(source, source + steps) for source in range(f...]
    reduce_scatter x2 -> x0, waiting for transfers between devices: 43.5 us -> none  [the longest x1 27.6 us: return_grid(): lax.psum_scatter(middle.astype(jnp.bfloat16), 'sub', scatter_dimension=0,...]
    scatter-add x6 -> x0, other arithmetic: 28 us -> none  [the longest x1 21.5 us: body(): jnp.zeros((grid_window.shape[0], latent), jnp.float32).at[grid_local]]
    ppermute x8 -> x0, starting transfers between devices: 23.2 us -> none  [the longest x4 11.9 us: from_behind(): lax.ppermute(value, axis, [(source, source + steps) for source in range(f...]
    all_gather x1 -> x0, waiting for transfers between devices: 20.4 us -> none  [fetch_grid(): block = lax.all_gather(projected, 'sub', axis=0, tiled=True)]
    dot_general x5 -> x8, matrix products: 6.66 us -> 18 us  [the longest x1 3.49 us: body(): projected = jnp.dot(hidden, w_src, preferred_element_type=F32).astype(BF16)]
  transfers between devices with their start and end apart: 12 -> 0, of which waited for: 7 -> 0; matrix products, arithmetic and copies ran while one was open for 5% -> 0% of each run, Pallas kernels for 0% -> 0%
where the time goes in v1:
time: 173 us; the launch traced here: 172 us
  Pallas kernels  85.7 us (50%)
  matrix products  45.5 us (26%)
  other arithmetic  22 us (13%)
  local copies, waits for them, and re-layouts  17.6 us (10%)
    pallas_call x1, Pallas kernels, sum_all(): pl.pallas_call(functools.partial(sum_kernel, bands, subs), out_shape=jax....  36.6 us
    pallas_call x2, Pallas kernels, fetch_window(): pl.pallas_call(functools.partial(window_kernel, bands, subs), out_shape=j...  25.3 us
    pallas_call x2, Pallas kernels, return_window(): pl.pallas_call(functools.partial(return_kernel, bands, subs), out_shape=j...  23.8 us
    dot_general x4, matrix products, first_contract(): lax.dot_general(left, right, (((0,), (0,)), ((), ())), preferred_element_...  15.9 us
    dot_general x4, matrix products, times_transpose(): lax.dot_general(left, right, (((1,), (1,)), ((), ())), preferred_element_...  11.6 us
    gather x1, local copies, waits for them, and re-layouts, body(): before = jnp.take(projected, grid_local, axis=0).astype(F32)  10.1 us
    convert_element_type x1, other arithmetic, body(): norm_grad = (centred_grad / spread).astype(BF16)  3.98 us
    reduce_sum x1, other arithmetic, body(): jnp.mean(incoming * normed, axis=-1, keepdims=True)  3.62 us

profile of v1, /device:TPU:13, one launch (start us, length us, event | category | flops | bytes accessed | tf_op | source)
XLA Modules:
  0.0 171.9 jit_solution(12652545955957042816)
XLA Ops:
  0.6 0.0 copy-start
  0.6 16.0 %window0.1 = bf16[6,227,512]{2,1,0:T(8,128)(2,1)} custom-call(bf16[227,512]{1,0:T(8,128)(2,1)} %x_ref.1), custom_call_target="tpu_custom_call" | custom-call | tf_op jit(solution)/shard_map/window0/pallas_call | solution.py:186
  16.7 2.5 %fusion.22 = f32[6,512,512]{2,1,0:T(8,128)S(1)} fusion(bf16[6,227,512]{2,1,0:T(8,128)(2,1)} %window0.1, bf16[227,512]{1,0:T(8,128)(2,1)} %param.13), kind=kOutput, calls=%fused_computation.50 | convolution fusion | flops 714080256 | bytes 7918592 | tf_op jit(solution)/shard_map/dot_general | solution.py:461
  19.2 1.7 %fusion.5 = bf16[3072,512]{1,0:T(8,128)(2,1)S(1)} fusion(f32[6,512,512]{2,1,0:T(8,128)S(1)} %fusion.22), kind=kLoop, calls=%fused_computation.12 | loop fusion | flops 7864320 | bytes 9437184 | tf_op jit(solution)/shard_map/convert_element_type | solution.py:464
  20.9 0.0 copy-start.16
  20.9 3.5 %convolution_convert_fusion = bf16[3072,512]{1,0:T(8,128)(2,1)} fusion(bf16[3072,512]{1,0:T(8,128)(2,1)S(1)} %fusion.5, bf16[512,512]{1,0:T(8,128)(2,1)S(1)} %copy-done), kind=kOutput, calls=%fused_computation.28 | convolution fusion | flops 1612185600 | bytes 6815744 | tf_op jit(solution)/shard_map/dot_general | solution.py:465
  24.4 0.1 copy.15
  24.5 0.1 reshape.142
  24.7 0.0 copy-start.11
  24.7 10.1 %gather_fusion = bf16[2560,512]{1,0:T(8,128)(2,1)S(1)} fusion(bf16[3072,512]{1,0:T(8,128)(2,1)} %convolution_convert_fusion, s32[3072]{0:T(1024)S(1)} %pad_clamp_fusion), kind=kCustom, calls=%fused_computation | custom fusion | bytes 5253120 | tf_op jit(solution)/shard_map/jit(_take)/gather | solution.py:468
  34.8 0.1 reshape.140
  34.9 0.6 copy-done.14
  35.5 1.3 fusion.32
  36.8 1.6 multiply_convert_fusion.1
  38.4 1.6 fusion.30
  40.0 0.9 multiply_reduce_fusion
  41.0 0.0 copy-start.12
  41.0 3.5 %subtract_divide_fusion = f32[2560,512]{1,0:T(8,128)} fusion(f32[2560,512]{1,0:T(8,128)S(1)} %get-tuple-element.10, f32[2560]{0:T(1024)S(1)} %add_sqrt_fusion, f32[2560]{0:T(1024)S(1)} %broadcast_multiply_fusion.1), kind=kLoop, calls=%fused_computation.26 | loop fusion | flops 2621440 | bytes 10506240 | tf_op jit(solution)/shard_map/div | solution.py:25
  44.5 3.4 %reduce_sum.67 = f32[64,512]{1,0:T(8,128)S(1)} reduce(f32[64,40,512]{2,1,0:T(8,128)} %bitcast.91, f32[]{:T(128)} %constant.53.clone.1), dimensions={1}, to_apply=%region_2.3 | reduce | flops 1277952 | bytes 5373956 | tf_op jit(solution)/shard_map/reduce_sum | solution.py:474
  47.9 0.9 add_convert_fusion.1
  48.7 1.9 %convolution_convert_fusion.5.x_ref = bf16[64,512]{1,0:T(8,128)(2,1)} fusion(bf16[64,512]{1,0:T(8,128)(2,1)S(1)} %add_convert_fusion.1, bf16[512,512]{1,0:T(8,128)(2,1)} %param.17), kind=kOutput, calls=%fused_computation.39 | convolution fusion | flops 33587200 | bytes 655360 | tf_op jit(solution)/shard_map/dot_general | solution.py:476
  50.6 9.3 %window1.1 = bf16[6,64,512]{2,1,0:T(8,128)(2,1)} custom-call(bf16[64,512]{1,0:T(8,128)(2,1)} %convolution_convert_fusion.5.x_ref), custom_call_target="tpu_custom_call" | custom-call | tf_op jit(solution)/shard_map/window1/pallas_call | solution.py:186
  59.9 1.9 %fusion.33 = f32[64,512]{1,0:T(8,128)} fusion(bf16[64,512]{1,0:T(8,128)(2,1)S(1)} %add_convert_fusion.1, bf16[512,512]{1,0:T(8,128)(2,1)} %param.18), kind=kOutput, calls=%fused_computation.74 | convolution fusion | flops 33554432 | bytes 720896 | tf_op jit(solution)/shard_map/dot_general | solution.py:477
  61.8 0.7 subtract_bitcast_fusion
  62.5 3.2 %fusion.27 = (bf16[64,512]{1,0:T(8,128)(2,1)}, f32[64,512]{1,0:T(8,128)}, bf16[6,64,512]{2,1,0:T(8,128)(2,1)}) fusion(f32[64,512]{1,0:T(8,128)S(1)} %convert_multiply_fusion, f32[64,512]{1,0:T(8,128)} %fusion.33, bf16[384,512,1]{1,0,2:T(8,128)(2,1)} %bitcast.96, s32[6,64]{1,0:T(8,128)S(1)} %subtract_bitcast_fusion), kind=kOutput, calls=%fused_computation.68 | convolution fusion | flops 153632768 | bytes 1246720 | tf_op jit(solution)/shard_map/dot_general | solution.py:481
  65.7 0.7 eq.57
  66.4 2.2 %convolution_convert_fusion.4 = bf16[384,512]{1,0:T(8,128)(2,1)} fusion(bf16[384,512]{1,0:T(8,128)(2,1)} %bitcast.98, s32[384]{0:T(512)S(1)} %eq.57), kind=kOutput, calls=%fused_computation.35 | convolution fusion | flops 151339008 | bytes 787968 | tf_op jit(solution)/shard_map/dot_general | solution.py:33
  68.7 8.3 %return2.1 = f32[64,512]{1,0:T(8,128)} custom-call(bf16[6,64,512]{2,1,0:T(8,128)(2,1)} %bitcast.97), custom_call_target="tpu_custom_call" | custom-call | tf_op jit(solution)/shard_map/return2/pallas_call | solution.py:298
  77.0 1.4 convolution_add_fusion.2
  78.3 1.5 fusion.31
  79.8 0.1 reduce_sum.71
  79.9 0.1 div.67
  80.0 3.6 %fusion.13 = f32[2560]{0:T(1024)S(1)} fusion(f32[64,512]{1,0:T(8,128)S(1)} %get-tuple-element.12, f32[2560]{0:T(1024)} %copy-done.12, f32[2560,512]{1,0:T(8,128)} %copy-done.1, f32[2560]{0:T(1024)S(1)} %broadcast_multiply_fusion.1), kind=kLoop, calls=%fused_computation.20 | loop fusion | flops 5240320 | bytes 5404672 | tf_op jit(solution)/shard_map/reduce_sum | solution.py:497
  83.6 0.0 copy-start.8
  83.7 4.0 %fusion.12 = bf16[2560,512]{1,0:T(8,128)(2,1)S(1)} fusion(f32[2560]{0:T(1024)S(1)} %broadcast_multiply_fusion, f32[2560]{0:T(1024)S(1)} %div.67, f32[64,512]{1,0:T(8,128)S(1)} %get-tuple-element.12, f32[2560]{0:T(1024)} %copy-done.12, f32[2560,512]{1,0:T(8,128)} %copy-done.1, f32[2560]{0:T(1024)S(1)} %broadcast_multiply_fusion.1), kind=kLoop, calls=%fused_computation.19 | loop fusion | flops 9175040 | bytes 8036352 | tf_op jit(solution)/shard_map/convert_element_type | solution.py:498
  87.7 3.2 %multiply_convert_fusion = bf16[2560,512]{1,0:T(8,128)(2,1)S(1)} fusion(bf16[2560,512]{1,0:T(8,128)(2,1)S(1)} %fusion.12, bf16[512,512]{1,0:T(8,128)(2,1)S(1)} %copy-done.8, f32[64,512]{1,0:T(8,128)S(1)} %fusion.32, bf16[2560,512]{1,0:T(8,128)(2,1)S(1)} %gather_fusion, pred[2560]{0:T(1024)(128)(4,1)S(1)} %compare_and_fusion), kind=kOutput, calls=%fused_computation.22 | convolution fusion | flops 1357905920 | bytes 8522240 | tf_op jit(solution)/shard_map/dot_general | solution.py:29
  90.9 10.4 %fusion.14 = bf16[3072,512]{1,0:T(8,128)(2,1)S(1)} fusion(bf16[2560,512]{1,0:T(8,128)(2,1)S(1)} %multiply_convert_fusion, s32[2560]{0:T(1024)S(1)} %copy-done.15), kind=kOutput, calls=%fused_computation.27 | convolution fusion | flops 8062500864 | bytes 5777408 | tf_op jit(solution)/shard_map/dot_general | solution.py:33
  101.3 1.8 %convolution_convert_fusion.2 = bf16[512,512]{1,0:T(8,128)(2,1)S(1)} fusion(bf16[3072,512]{1,0:T(8,128)(2,1)S(1)} %copy-done.6, bf16[3072,512]{1,0:T(8,128)(2,1)S(1)} %fusion.14), kind=kOutput, calls=%fused_computation.32 | convolution fusion | flops 1610874880 | bytes 6815744 | tf_op jit(solution)/shard_map/dot_general | solution.py:33
  103.1 1.0 copy-done.4
  104.1 1.5 convolution_convert_fusion.3
  105.7 1.0 pad_maximum_fusion
  106.7 36.6 %sum4.1 = bf16[32,32,512]{2,1,0:T(8,128)(2,1)} custom-call(bf16[32,32,512]{2,1,0:T(8,128)(2,1)} %bitcast.92), custom_call_target="tpu_custom_call" | custom-call | tf_op jit(solution)/shard_map/sum4/pallas_call | solution.py:424
  143.3 2.8 %fusion.29 = (f32[16,32,512]{2,1,0:T(8,128)}, f32[16,32,512]{2,1,0:T(8,128)}) fusion(bf16[32,32,512]{2,1,0:T(8,128)(2,1)} %sum4.1), kind=kLoop, calls=%fused_computation.70 | loop fusion | bytes 4194304 | tf_op jit(solution)/shard_map/slice | solution.py:514
  146.1 5.5 %fusion.9 = bf16[3072,512]{1,0:T(8,128)(2,1)S(1)} fusion(f32[6,512,512]{2,1,0:T(8,128)} %copy-done.2, bf16[3072,512]{1,0:T(8,128)(2,1)} %copy-done.18, bf16[512,512]{1,0:T(8,128)(2,1)S(1)} %copy-done), kind=kOutput, calls=%fused_computation.16 | convolution fusion | flops 1624768512 | bytes 13107200 | tf_op jit(solution)/shard_map/dot_general | solution.py:29
  151.7 2.2 %fusion.15.g_ref = bf16[6,227,512]{2,1,0:T(8,128)(2,1)} fusion(bf16[6,512,512]{2,1,0:T(8,128)(2,1)S(1)} %bitcast.93, bf16[227,512]{1,0:T(8,128)(2,1)S(1)} %copy-done.9), kind=kOutput, calls=%fused_computation.31 | convolution fusion | flops 714777600 | bytes 4772864 | tf_op jit(solution)/shard_map/dot_general | solution.py:504
  153.8 15.5 %return3.1 = f32[227,512]{1,0:T(8,128)} custom-call(bf16[6,227,512]{2,1,0:T(8,128)(2,1)} %fusion.15.g_ref), custom_call_target="tpu_custom_call" | custom-call | tf_op jit(solution)/shard_map/return3/pallas_call | solution.py:298
  169.4 0.6 add_convert_fusion
  170.0 1.8 %copy.18 = f32[227,512]{1,0:T(8,128)} copy(f32[227,512]{1,0:T(8,128)} %return3.1) | data formatting | bytes 929792
  (40 shorter events, 0.2 us)
Async XLA Ops:
  0.6 20.3 %copy-start = (bf16[512,512]{1,0:T(8,128)(2,1)S(1)}, bf16[512,512]{1,0:T(8,128)(2,1)}, u32[]{:S(2)}) copy-start(bf16[512,512]{1,0:T(8,128)(2,1)} %param.14) | copy-start | bytes 1572868
  19.2 5.3 %copy-start.2 = (f32[6,512,512]{2,1,0:T(8,128)}, f32[6,512,512]{2,1,0:T(8,128)S(1)}, u32[]{:S(2)}) copy-start(f32[6,512,512]{2,1,0:T(8,128)S(1)} %fusion.22) | copy-start | bytes 18874372
  20.9 3.5 %copy-start.5 = (bf16[3072,512]{1,0:T(8,128)(2,1)}, bf16[3072,512]{1,0:T(8,128)(2,1)S(1)}, u32[]{:S(2)}) copy-start(bf16[3072,512]{1,0:T(8,128)(2,1)S(1)} %fusion.5) | copy-start | bytes 9437188
  20.9 3.5 %copy-start.16 = (s32[64,40]{0,1:T(8,128)S(1)}, s32[64,40]{0,1:T(8,128)}, u32[]{:S(2)}) copy-start(s32[64,40]{0,1:T(8,128)} %param.19) | copy-start | bytes 30724
  24.7 10.8 %copy-start.11 = (bf16[64,512]{1,0:T(8,128)(2,1)S(1)}, bf16[64,512]{1,0:T(8,128)(2,1)}, u32[]{:S(2)}) copy-start(bf16[64,512]{1,0:T(8,128)(2,1)} %param.12) | copy-start | bytes 196612
  34.9 0.6 copy-start.14
  35.5 2.9 %copy-start.7 = (bf16[512,512]{1,0:T(8,128)(2,1)S(1)}, bf16[512,512]{1,0:T(8,128)(2,1)}, u32[]{:S(2)}) copy-start(bf16[512,512]{1,0:T(8,128)(2,1)} %param.16) | copy-start | bytes 1572868
  38.4 1.6 copy-start.3
  40.0 4.5 %copy-start.1 = (f32[2560,512]{1,0:T(8,128)}, f32[2560,512]{1,0:T(8,128)S(1)}, u32[]{:S(2)}) copy-start(f32[2560,512]{1,0:T(8,128)S(1)} %get-tuple-element.10) | copy-start | bytes 15728644
  41.0 3.5 %copy-start.12 = (f32[2560]{0:T(1024)}, f32[2560]{0:T(1024)S(1)}, u32[]{:S(2)}) copy-start(f32[2560]{0:T(1024)S(1)} %add_sqrt_fusion) | copy-start | bytes 30724
  44.5 18.0 %copy-start.10 = (bf16[64,512]{1,0:T(8,128)(2,1)S(1)}, bf16[64,512]{1,0:T(8,128)(2,1)}, u32[]{:S(2)}) copy-start(bf16[64,512]{1,0:T(8,128)(2,1)} %param.21) | copy-start | bytes 196612
  62.5 3.2 %copy-start.17 = (s32[6,64]{1,0:T(8,128)}, s32[6,64]{1,0:T(8,128)S(1)}, u32[]{:S(2)}) copy-start(s32[6,64]{1,0:T(8,128)S(1)} %subtract_bitcast_fusion) | copy-start | bytes 4612
  83.6 4.0 %copy-start.8 = (bf16[512,512]{1,0:T(8,128)(2,1)S(1)}, bf16[512,512]{1,0:T(8,128)(2,1)}, u32[]{:S(2)}) copy-start(bf16[512,512]{1,0:T(8,128)(2,1)} %param.16) | copy-start | bytes 1572868
  87.7 3.2 %copy-start.15 = (s32[2560]{0:T(1024)S(1)}, s32[2560]{0:T(1024)}, u32[]{:S(2)}) copy-start(s32[2560]{0:T(1024)} %copy-done.14) | copy-start | bytes 30724
  90.9 10.4 %copy-start.6 = (bf16[3072,512]{1,0:T(8,128)(2,1)S(1)}, bf16[3072,512]{1,0:T(8,128)(2,1)}, u32[]{:S(2)}) copy-start(bf16[3072,512]{1,0:T(8,128)(2,1)} %copy-done.5) | copy-start | bytes 9437188
  101.3 1.8 %copy-start.18 = (bf16[3072,512]{1,0:T(8,128)(2,1)}, bf16[3072,512]{1,0:T(8,128)(2,1)S(1)}, u32[]{:S(2)}) copy-start(bf16[3072,512]{1,0:T(8,128)(2,1)S(1)} %fusion.14) | copy-start | bytes 9437188
  101.3 2.9 %copy-start.4 = (bf16[2560,512]{1,0:T(8,128)(2,1)S(1)}, bf16[2560,512]{1,0:T(8,128)(2,1)}, u32[]{:S(2)}) copy-start(bf16[2560,512]{1,0:T(8,128)(2,1)} %copy-done.3) | copy-start | bytes 7864324
  146.1 5.6 %copy-start.9 = (bf16[227,512]{1,0:T(8,128)(2,1)S(1)}, bf16[227,512]{1,0:T(8,128)(2,1)}, u32[]{:S(2)}) copy-start(bf16[227,512]{1,0:T(8,128)(2,1)} %param.13) | copy-start | bytes 697348
  151.7 17.7 %copy-start.13 = (f32[64,512]{1,0:T(8,128)S(1)}, f32[64,512]{1,0:T(8,128)}, u32[]{:S(2)}) copy-start(f32[64,512]{1,0:T(8,128)} %get-tuple-element.5) | copy-start | bytes 393220

commit v2 on v1

--- a/solution.py
+++ b/solution.py
@@ -198,11 +198,10 @@
     )(block)
 
 
-def return_kernel(
+def return_stream(
     bands, subs, g_ref, o_ref, pairbuf, stage, far, edge, send1, recv1, send2, far_sem, edge_sem
 ):
     band, me, core, chip, partner, chips = place(subs)
-    near_barrier(bands, subs, band, me)
     order = list(range(1, chips)) + [chips, 0]
 
     def slot_of(step, which):
@@ -220,6 +219,7 @@
             (band, partner),
         )
         swaps[step].start()
+    yield
 
     def combined(step):
         swaps[step].wait_recv()
@@ -255,6 +255,7 @@
     def _():
         border(band + 1, 0).start()
 
+    yield
     total = combined(0)
     for step, copy in enumerate(across):
         copy.wait_recv()
@@ -292,6 +293,28 @@
         border(band + 1, 0).wait_send()
 
 
+def return_kernel(bands, subs, *refs):
+    band, me = (lax.axis_index("band"), lax.axis_index("sub"))
+    near_barrier(bands, subs, band, me)
+    for _ in return_stream(bands, subs, *refs):
+        pass
+
+
+def return_scratch(chips, block):
+    dma = pltpu.SemaphoreType.DMA
+    return [
+        pltpu.VMEM((chips + 1,) + block, BF16),
+        pltpu.VMEM((chips,) + block, BF16),
+        pltpu.VMEM((chips,) + block, BF16),
+        pltpu.VMEM((chips,) + block, BF16),
+        dma((chips + 1,)),
+        dma((chips + 1,)),
+        dma((chips,)),
+        dma((chips,)),
+        dma((chips,)),
+    ]
+
+
 def return_window(slots, bands, subs, ident):
     chips = subs // 2
     block = slots.shape[1:]
@@ -300,33 +323,16 @@
         out_shape=jax.ShapeDtypeStruct(block, F32),
         in_specs=[VMEM],
         out_specs=VMEM,
-        scratch_shapes=[
-            pltpu.VMEM((chips + 1,) + block, BF16),
-            pltpu.VMEM((chips,) + block, BF16),
-            pltpu.VMEM((chips,) + block, BF16),
-            pltpu.VMEM((chips,) + block, BF16),
-            pltpu.SemaphoreType.DMA((chips + 1,)),
-            pltpu.SemaphoreType.DMA((chips + 1,)),
-            pltpu.SemaphoreType.DMA((chips,)),
-            pltpu.SemaphoreType.DMA((chips,)),
-            pltpu.SemaphoreType.DMA((chips,)),
-        ],
+        scratch_shapes=return_scratch(chips, block),
         compiler_params=pltpu.CompilerParams(collective_id=ident, has_side_effects=True),
         name=f"return{ident}",
     )(slots)
 
 
-def sum_kernel(
+def sum_stream(
     bands, subs, v_ref, o_ref, r1, a1, r2, a2, r3, s1, q1, s2, q2, s3, q3, s4, q4, s5, q5, s6, q6
 ):
     band, me, core, chip, partner, chips = place(subs)
-    barrier = pltpu.get_barrier_semaphore()
-    greet(barrier, (band, partner))
-    for k in range(1, chips):
-        greet(barrier, (band, 2 * lax.rem(chip + k, chips) + core))
-    for i in range(1, bands):
-        greet(barrier, (lax.rem(band + i, bands), me))
-    pl.semaphore_wait(barrier, chips + bands - 1)
     half = chips * bands
 
     def part(which, step):
@@ -340,6 +346,7 @@
         )
         swaps[step].start()
     waits = list(swaps.values())
+    yield
     across = []
     for step in order:
         swaps[step].wait_recv()
@@ -355,6 +362,7 @@
             )
             copy.start()
             across.append(copy)
+    yield
     for step, copy in enumerate(across):
         copy.wait_recv()
         total = total + r2[step + 1].astype(F32)
@@ -366,6 +374,7 @@
         copy = remote(a2.at[goal], r3.at[i], s3.at[i], q3.at[i], (goal, me))
         copy.start()
         spread.append(copy)
+    yield
     total = a2[band].astype(F32)
     for i, copy in enumerate(spread):
         copy.wait_recv()
@@ -380,6 +389,7 @@
         )
         copy.start()
         spread.append(copy)
+    yield
     for copy in spread:
         copy.wait_recv()
     waits += spread
@@ -400,6 +410,7 @@
         )
     ]
     relays[0].start()
+    yield
     for step, copy in enumerate(across):
         copy.wait_recv()
         rows = part(core, chips - step - 1)
@@ -408,38 +419,81 @@
         )
         relay.start()
         relays.append(relay)
+    yield
     for relay in relays:
         relay.wait_recv()
     for copy in waits + across + relays:
         copy.wait_send()
 
 
-def sum_all(value, bands, subs, ident):
+def sum_scratch(chips, bands, deep, latent):
+    dma = pltpu.SemaphoreType.DMA
+    return (
+        [pltpu.VMEM((chips, bands, deep, latent), BF16)] * 3
+        + [pltpu.VMEM((bands, deep, latent), BF16)] * 2
+        + [dma((chips,))] * 4
+        + [dma((bands,))] * 4
+        + [dma((chips,))] * 4
+    )
+
+
+def tail_kernel(bands, subs, streams, *refs):
+    band, me = (lax.axis_index("band"), lax.axis_index("sub"))
+    barrier = pltpu.get_barrier_semaphore()
+    for step in range(1, subs):
+        greet(barrier, (band, lax.rem(me + step, subs)))
+
+    @pl.when(band > 0)
+    def _():
+        for other in range(subs):
+            greet(barrier, (band - 1, other))
+
+    @pl.when(band < bands - 1)
+    def _():
+        for other in range(subs):
+            greet(barrier, (band + 1, other))
+
+    for i in range(1, bands):
+        goal = lax.rem(band + i, bands)
+
+        @pl.when((goal != band + 1) & (goal != band - 1))
+        def _():
+            greet(barrier, (goal, me))
+
+    sides = jnp.minimum(band, 1) + jnp.minimum(bands - 1 - band, 1)
+    pl.semaphore_wait(barrier, subs + bands - 2 + (subs - 1) * sides)
+    count = streams + 1
+    ins, outs, scratch = (refs[:count], refs[count : 2 * count], refs[2 * count :])
+    active = [
+        sum_stream(bands, subs, ins[i], outs[i], *scratch[17 * i : 17 * i + 17])
+        for i in range(streams)
+    ]
+    active.append(return_stream(bands, subs, ins[-1], outs[-1], *scratch[17 * streams :]))
+    while active:
+        active = [stream for stream in active if next(stream, True) is None]
+
+
+def tail(values, slots, bands, subs, ident):
     chips = subs // 2
     count = bands * subs
-    rows, latent = value.shape
+    rows, latent = values[0].shape
     deep = rows // count
-    value = value.reshape(count, deep, latent)
-    dma = pltpu.SemaphoreType.DMA
-    total = pl.pallas_call(
-        functools.partial(sum_kernel, bands, subs),
-        out_shape=jax.ShapeDtypeStruct(value.shape, BF16),
-        in_specs=[VMEM],
-        out_specs=VMEM,
-        scratch_shapes=[
-            pltpu.VMEM((chips, bands, deep, latent), BF16),
-            pltpu.VMEM((chips, bands, deep, latent), BF16),
-            pltpu.VMEM((chips, bands, deep, latent), BF16),
-            pltpu.VMEM((bands, deep, latent), BF16),
-            pltpu.VMEM((bands, deep, latent), BF16),
-        ]
-        + [dma((chips,)), dma((chips,))] * 2
-        + [dma((bands,)), dma((bands,))] * 2
-        + [dma((chips,)), dma((chips,))] * 2,
+    block = slots.shape[1:]
+    shape = (count, deep, latent)
+    scratch = []
+    for _ in values:
+        scratch += sum_scratch(chips, bands, deep, latent)
+    results = pl.pallas_call(
+        functools.partial(tail_kernel, bands, subs, len(values)),
+        out_shape=[jax.ShapeDtypeStruct(shape, BF16)] * len(values)
+        + [jax.ShapeDtypeStruct(block, F32)],
+        in_specs=[VMEM] * (len(values) + 1),
+        out_specs=[VMEM] * (len(values) + 1),
+        scratch_shapes=scratch + return_scratch(chips, block),
         compiler_params=pltpu.CompilerParams(collective_id=ident, has_side_effects=True),
-        name=f"sum{ident}",
-    )(value)
-    return total.reshape(rows, latent)
+        name="tail",
+    )(*[value.reshape(shape) for value in values], slots)
+    return [result.reshape(rows, latent) for result in results[:-1]] + [results[-1]]
 
 
 def one_hot(index, count):
@@ -508,10 +562,10 @@
         preferred_element_type=F32,
     )
     grid_part = jnp.swapaxes(grid_part, 0, 1).astype(BF16)
-    grid_grad = return_window(grid_part, bands, subs, 3)
-    parts = jnp.concatenate([src_part, edge_part], axis=0).astype(BF16)
-    sums = sum_all(parts, bands, subs, 4).astype(F32)
-    return (mesh_out, grid_grad, sums[:latent], sums[latent:])
+    src_grad, edge_grad, grid_grad = tail(
+        [src_part.astype(BF16), edge_part.astype(BF16)], grid_part, bands, subs, 3
+    )
+    return (mesh_out, grid_grad, src_grad.astype(F32), edge_grad.astype(F32))
 
 
 def solution(mesh):

time: 173 us -> 156 us (0.902)
  Pallas kernels: 85.7 us -> 72.2 us
  local copies, waits for them, and re-layouts: 17.6 us -> 13.7 us
  other arithmetic: 22 us -> 23.8 us
    pallas_call x2 -> x1, Pallas kernels: 23.8 us -> 8.29 us  [return_window(): pl.pallas_call(functools.partial(return_kernel, bands, subs), out_shape=j...]
    convert_element_type x0 -> x1, other arithmetic: none -> 2.81 us  [body(): return (mesh_out, grid_grad, src_grad.astype(F32), edge_grad.astype(F32))]
    slice x1 -> x0, local copies, waits for them, and re-layouts: 2.8 us -> none  [body(): return (mesh_out, grid_grad, sums[:latent], sums[latent:])]
    dot_general x4, matrix products: 11.6 us -> 9.34 us  [times_transpose(): lax.dot_general(left, right, (((1,), (1,)), ((), ())), preferred_element_...]
    pallas_call x1, Pallas kernels: 36.6 us -> 38.6 us  [tail(): pl.pallas_call(functools.partial(tail_kernel, bands, subs, len(values)),...]
    unnamed x39 -> x41, local copies, waits for them, and re-layouts: 3.54 us -> 2.51 us
where the time goes in v2:
time: 156 us
  Pallas kernels  72.2 us (46%)
  matrix products  44.9 us (29%)
  other arithmetic  23.8 us (15%)
  local copies, waits for them, and re-layouts  13.7 us (9%)
    pallas_call x1, Pallas kernels, tail(): pl.pallas_call(functools.partial(tail_kernel, bands, subs, len(values)),...  38.6 us
    pallas_call x2, Pallas kernels, fetch_window(): pl.pallas_call(functools.partial(window_kernel, bands, subs), out_shape=j...  25.3 us
    dot_general x4, matrix products, first_contract(): lax.dot_general(left, right, (((0,), (0,)), ((), ())), preferred_element_...  17.5 us
    gather x1, local copies, waits for them, and re-layouts, body(): before = jnp.take(projected, grid_local, axis=0).astype(F32)  10.1 us
    dot_general x4, matrix products, times_transpose(): lax.dot_general(left, right, (((1,), (1,)), ((), ())), preferred_element_...  9.34 us
    pallas_call x1, Pallas kernels, return_window(): pl.pallas_call(functools.partial(return_kernel, bands, subs), out_shape=j...  8.29 us
    convert_element_type x1, other arithmetic, body(): norm_grad = (centred_grad / spread).astype(BF16)  3.98 us
    reduce_sum x1, other arithmetic, body(): jnp.mean(incoming * normed, axis=-1, keepdims=True)  3.62 us

profile of v2, /device:TPU:13, one launch (start us, length us, event | category | flops | bytes accessed | tf_op | source)
XLA Modules:
  0.0 155.7 jit_solution(5692694579733306969)
XLA Ops:
  0.6 0.0 copy-start
  0.6 16.1 %window0.1 = bf16[6,227,512]{2,1,0:T(8,128)(2,1)} custom-call(bf16[227,512]{1,0:T(8,128)(2,1)} %x_ref.1), custom_call_target="tpu_custom_call" | custom-call | tf_op jit(solution)/shard_map/window0/pallas_call | solution.py:186
  16.7 2.5 %fusion.22 = f32[6,512,512]{2,1,0:T(8,128)S(1)} fusion(bf16[6,227,512]{2,1,0:T(8,128)(2,1)} %window0.1, bf16[227,512]{1,0:T(8,128)(2,1)} %param.13), kind=kOutput, calls=%fused_computation.51 | convolution fusion | flops 714080256 | bytes 7918592 | tf_op jit(solution)/shard_map/dot_general | solution.py:515
  19.2 1.7 %fusion.5 = bf16[3072,512]{1,0:T(8,128)(2,1)S(1)} fusion(f32[6,512,512]{2,1,0:T(8,128)S(1)} %fusion.22), kind=kLoop, calls=%fused_computation.12 | loop fusion | flops 7864320 | bytes 9437184 | tf_op jit(solution)/shard_map/convert_element_type | solution.py:518
  20.9 0.0 copy-start.16
  21.0 3.5 %convolution_convert_fusion = bf16[3072,512]{1,0:T(8,128)(2,1)} fusion(bf16[3072,512]{1,0:T(8,128)(2,1)S(1)} %fusion.5, bf16[512,512]{1,0:T(8,128)(2,1)S(1)} %copy-done), kind=kOutput, calls=%fused_computation.28 | convolution fusion | flops 1612185600 | bytes 6815744 | tf_op jit(solution)/shard_map/dot_general | solution.py:519
  24.5 0.1 copy.15
  24.5 0.1 reshape.147
  24.7 0.0 copy-start.11
  24.7 10.1 %gather_fusion = bf16[2560,512]{1,0:T(8,128)(2,1)S(1)} fusion(bf16[3072,512]{1,0:T(8,128)(2,1)} %convolution_convert_fusion, s32[3072]{0:T(1024)S(1)} %pad_clamp_fusion), kind=kCustom, calls=%fused_computation | custom fusion | bytes 5253120 | tf_op jit(solution)/shard_map/jit(_take)/gather | solution.py:522
  34.8 0.1 reshape.145
  34.9 0.6 copy-done.14
  35.5 1.3 fusion.31
  36.8 1.6 %multiply_convert_fusion.1 = bf16[2560,512]{1,0:T(8,128)(2,1)S(1)} fusion(f32[64,512]{1,0:T(8,128)S(1)} %fusion.31, bf16[2560,512]{1,0:T(8,128)(2,1)S(1)} %gather_fusion, pred[2560]{0:T(1024)(128)(4,1)S(1)} %compare_and_fusion), kind=kLoop, calls=%fused_computation.24 | loop fusion | flops 10485760 | bytes 5376512 | tf_op jit(solution)/shard_map/convert_element_type | solution.py:526
  38.4 1.6 %fusion.29 = (f32[2560]{0:T(1024)S(1)}, f32[2560,512]{1,0:T(8,128)S(1)}) fusion(bf16[2560,512]{1,0:T(8,128)(2,1)S(1)} %multiply_convert_fusion.1, bf16[512,512]{1,0:T(8,128)(2,1)S(1)} %copy-done.7), kind=kOutput, calls=%fused_computation.71 | convolution fusion | flops 1343485440 | bytes 8398848 | tf_op jit(solution)/shard_map/dot_general | solution.py:527
  40.0 0.9 multiply_reduce_fusion
  41.0 0.0 copy-start.12
  41.0 3.5 %subtract_divide_fusion = f32[2560,512]{1,0:T(8,128)} fusion(f32[2560,512]{1,0:T(8,128)S(1)} %get-tuple-element.14, f32[2560]{0:T(1024)S(1)} %add_sqrt_fusion, f32[2560]{0:T(1024)S(1)} %broadcast_multiply_fusion.1), kind=kLoop, calls=%fused_computation.26 | loop fusion | flops 2621440 | bytes 10506240 | tf_op jit(solution)/shard_map/div | solution.py:25
  44.4 3.4 %reduce_sum.67 = f32[64,512]{1,0:T(8,128)S(1)} reduce(f32[64,40,512]{2,1,0:T(8,128)} %bitcast.98, f32[]{:T(128)} %constant.53.clone.1), dimensions={1}, to_apply=%region_2.3 | reduce | flops 1277952 | bytes 5373956 | tf_op jit(solution)/shard_map/reduce_sum | solution.py:528
  47.8 0.9 add_convert_fusion.1
  48.7 1.9 %convolution_convert_fusion.5.x_ref = bf16[64,512]{1,0:T(8,128)(2,1)} fusion(bf16[64,512]{1,0:T(8,128)(2,1)S(1)} %add_convert_fusion.1, bf16[512,512]{1,0:T(8,128)(2,1)} %param.17), kind=kOutput, calls=%fused_computation.39 | convolution fusion | flops 33587200 | bytes 655360 | tf_op jit(solution)/shard_map/dot_general | solution.py:530
  50.6 9.3 %window1.1 = bf16[6,64,512]{2,1,0:T(8,128)(2,1)} custom-call(bf16[64,512]{1,0:T(8,128)(2,1)} %convolution_convert_fusion.5.x_ref), custom_call_target="tpu_custom_call" | custom-call | tf_op jit(solution)/shard_map/window1/pallas_call | solution.py:186
  59.9 1.9 %fusion.32 = f32[64,512]{1,0:T(8,128)} fusion(bf16[64,512]{1,0:T(8,128)(2,1)S(1)} %add_convert_fusion.1, bf16[512,512]{1,0:T(8,128)(2,1)} %param.18), kind=kOutput, calls=%fused_computation.74 | convolution fusion | flops 33554432 | bytes 720896 | tf_op jit(solution)/shard_map/dot_general | solution.py:531
  61.8 0.7 subtract_bitcast_fusion
  62.5 3.2 %fusion.27 = (bf16[64,512]{1,0:T(8,128)(2,1)}, f32[64,512]{1,0:T(8,128)}, bf16[6,64,512]{2,1,0:T(8,128)(2,1)}) fusion(f32[64,512]{1,0:T(8,128)S(1)} %convert_multiply_fusion, f32[64,512]{1,0:T(8,128)} %fusion.32, bf16[384,512,1]{1,0,2:T(8,128)(2,1)} %bitcast.102, s32[6,64]{1,0:T(8,128)S(1)} %subtract_bitcast_fusion), kind=kOutput, calls=%fused_computation.69 | convolution fusion | flops 153632768 | bytes 1246720 | tf_op jit(solution)/shard_map/dot_general | solution.py:535
  65.7 0.7 eq.57
  66.4 2.2 %convolution_convert_fusion.4 = bf16[384,512]{1,0:T(8,128)(2,1)} fusion(bf16[384,512]{1,0:T(8,128)(2,1)} %bitcast.104, s32[384]{0:T(512)S(1)} %eq.57), kind=kOutput, calls=%fused_computation.35 | convolution fusion | flops 151339008 | bytes 787968 | tf_op jit(solution)/shard_map/dot_general | solution.py:33
  68.6 8.3 %return2.1 = f32[64,512]{1,0:T(8,128)} custom-call(bf16[6,64,512]{2,1,0:T(8,128)(2,1)} %bitcast.103), custom_call_target="tpu_custom_call" | custom-call | tf_op jit(solution)/shard_map/return2/pallas_call | solution.py:321
  76.9 1.4 convolution_add_fusion.2
  78.3 1.5 fusion.30
  79.8 0.1 reduce_sum.71
  79.9 0.1 div.67
  80.0 3.6 %fusion.13 = f32[2560]{0:T(1024)S(1)} fusion(f32[64,512]{1,0:T(8,128)S(1)} %get-tuple-element.16, f32[2560]{0:T(1024)} %copy-done.12, f32[2560,512]{1,0:T(8,128)} %copy-done.1, f32[2560]{0:T(1024)S(1)} %broadcast_multiply_fusion.1), kind=kLoop, calls=%fused_computation.20 | loop fusion | flops 5240320 | bytes 5404672 | tf_op jit(solution)/shard_map/reduce_sum | solution.py:551
  83.6 0.0 copy-start.8
  83.6 4.0 %fusion.12 = bf16[2560,512]{1,0:T(8,128)(2,1)S(1)} fusion(f32[2560]{0:T(1024)S(1)} %broadcast_multiply_fusion, f32[2560]{0:T(1024)S(1)} %div.67, f32[64,512]{1,0:T(8,128)S(1)} %get-tuple-element.16, f32[2560]{0:T(1024)} %copy-done.12, f32[2560,512]{1,0:T(8,128)} %copy-done.1, f32[2560]{0:T(1024)S(1)} %broadcast_multiply_fusion.1), kind=kLoop, calls=%fused_computation.19 | loop fusion | flops 9175040 | bytes 8036352 | tf_op jit(solution)/shard_map/convert_element_type | solution.py:552
  87.6 0.0 slice-start
  87.7 3.2 %multiply_convert_fusion = bf16[2560,512]{1,0:T(8,128)(2,1)S(1)} fusion(bf16[2560,512]{1,0:T(8,128)(2,1)S(1)} %fusion.12, bf16[512,512]{1,0:T(8,128)(2,1)S(1)} %copy-done.8, f32[64,512]{1,0:T(8,128)S(1)} %fusion.31, bf16[2560,512]{1,0:T(8,128)(2,1)S(1)} %gather_fusion, pred[2560]{0:T(1024)(128)(4,1)S(1)} %compare_and_fusion), kind=kOutput, calls=%fused_computation.22 | convolution fusion | flops 1357905920 | bytes 8522240 | tf_op jit(solution)/shard_map/dot_general | solution.py:29
  90.9 0.0 slice-start.1
  90.9 10.4 %fusion.14 = bf16[3072,512]{1,0:T(8,128)(2,1)S(1)} fusion(bf16[2560,512]{1,0:T(8,128)(2,1)S(1)} %multiply_convert_fusion, s32[2560]{0:T(1024)S(1)} %copy-done.15), kind=kOutput, calls=%fused_computation.27 | convolution fusion | flops 8062500864 | bytes 5777408 | tf_op jit(solution)/shard_map/dot_general | solution.py:33
  101.3 0.0 copy-start.9
  101.3 3.3 %fusion.9 = bf16[3072,512]{1,0:T(8,128)(2,1)S(1)} fusion(f32[6,512,512]{2,1,0:T(8,128)S(1)} %bitcast.97, bf16[3072,512]{1,0:T(8,128)(2,1)S(1)} %fusion.14, bf16[512,512]{1,0:T(8,128)(2,1)S(1)} %copy-done), kind=kOutput, calls=%fused_computation.16 | convolution fusion | flops 1624768512 | bytes 13107200 | tf_op jit(solution)/shard_map/dot_general | solution.py:29
  104.6 2.2 %fusion.15.refs_2_ = bf16[6,227,512]{2,1,0:T(8,128)(2,1)} fusion(bf16[6,512,512]{2,1,0:T(8,128)(2,1)S(1)} %bitcast.99, bf16[227,512]{1,0:T(8,128)(2,1)S(1)} %copy-done.9), kind=kOutput, calls=%fused_computation.31 | convolution fusion | flops 714777600 | bytes 4772864 | tf_op jit(solution)/shard_map/dot_general | solution.py:558
  106.8 2.3 %convolution_convert_fusion.3 = bf16[512,512]{1,0:T(8,128)(2,1)} fusion(bf16[2560,512]{1,0:T(8,128)(2,1)S(1)} %copy-done.4, bf16[2560,512]{1,0:T(8,128)(2,1)S(1)} %fusion.12), kind=kOutput, calls=%fused_computation.33 | convolution fusion | flops 1342439424 | bytes 5767168 | tf_op jit(solution)/shard_map/dot_general | solution.py:33
  109.1 2.6 %convolution_convert_fusion.2 = bf16[512,512]{1,0:T(8,128)(2,1)} fusion(bf16[3072,512]{1,0:T(8,128)(2,1)S(1)} %copy-done.6, bf16[3072,512]{1,0:T(8,128)(2,1)S(1)} %fusion.14), kind=kOutput, calls=%fused_computation.32 | convolution fusion | flops 1610874880 | bytes 6815744 | tf_op jit(solution)/shard_map/dot_general | solution.py:33
  111.7 38.6 %tail.1 = (bf16[32,16,512]{2,1,0:T(8,128)(2,1)}, bf16[32,16,512]{2,1,0:T(8,128)(2,1)}, f32[227,512]{1,0:T(8,128)}) custom-call(bf16[32,16,512]{2,1,0:T(8,128)(2,1)} %bitcast.101, bf16[32,16,512]{2,1,0:T(8,128)(2,1)} %bitcast.100, bf16[6,227,512]{2,1,0:T(8,128)(2,1)} %fusion.15.refs_2_), custom_call_target="tpu_custom_call" | custom-call | tf_op jit(solution)/shard_map/tail/pallas_call | solution.py:486
  150.4 2.8 %bitcast_convert_fusion = (f32[512,512]{1,0:T(8,128)}, f32[512,512]{1,0:T(8,128)}) fusion(bf16[32,16,512]{2,1,0:T(8,128)(2,1)} %get-tuple-element.9, bf16[32,16,512]{2,1,0:T(8,128)(2,1)} %get-tuple-element.8), kind=kLoop, calls=%fused_computation.46 | loop fusion | flops 524288 | bytes 3145728 | tf_op jit(solution)/shard_map/convert_element_type | solution.py:568
  153.2 0.6 add_convert_fusion
  153.8 1.8 %copy.18 = f32[227,512]{1,0:T(8,128)} copy(f32[227,512]{1,0:T(8,128)} %get-tuple-element.24) | data formatting | bytes 929792
  (41 shorter events, 0.2 us)
Async XLA Ops:
  0.6 20.3 %copy-start = (bf16[512,512]{1,0:T(8,128)(2,1)S(1)}, bf16[512,512]{1,0:T(8,128)(2,1)}, u32[]{:S(2)}) copy-start(bf16[512,512]{1,0:T(8,128)(2,1)} %param.14) | copy-start | bytes 1572868
  19.2 5.3 %copy-start.2 = (f32[6,512,512]{2,1,0:T(8,128)}, f32[6,512,512]{2,1,0:T(8,128)S(1)}, u32[]{:S(2)}) copy-start(f32[6,512,512]{2,1,0:T(8,128)S(1)} %fusion.22) | copy-start | bytes 18874372
  20.9 3.5 %copy-start.5 = (bf16[3072,512]{1,0:T(8,128)(2,1)}, bf16[3072,512]{1,0:T(8,128)(2,1)S(1)}, u32[]{:S(2)}) copy-start(bf16[3072,512]{1,0:T(8,128)(2,1)S(1)} %fusion.5) | copy-start | bytes 9437188
  20.9 3.5 %copy-start.16 = (s32[64,40]{0,1:T(8,128)S(1)}, s32[64,40]{0,1:T(8,128)}, u32[]{:S(2)}) copy-start(s32[64,40]{0,1:T(8,128)} %param.19) | copy-start | bytes 30724
  24.7 10.8 %copy-start.11 = (bf16[64,512]{1,0:T(8,128)(2,1)S(1)}, bf16[64,512]{1,0:T(8,128)(2,1)}, u32[]{:S(2)}) copy-start(bf16[64,512]{1,0:T(8,128)(2,1)} %param.12) | copy-start | bytes 196612
  34.9 0.6 copy-start.14
  35.5 2.9 %copy-start.7 = (bf16[512,512]{1,0:T(8,128)(2,1)S(1)}, bf16[512,512]{1,0:T(8,128)(2,1)}, u32[]{:S(2)}) copy-start(bf16[512,512]{1,0:T(8,128)(2,1)} %param.16) | copy-start | bytes 1572868
  38.4 1.6 %copy-start.3 = (bf16[2560,512]{1,0:T(8,128)(2,1)}, bf16[2560,512]{1,0:T(8,128)(2,1)S(1)}, u32[]{:S(2)}) copy-start(bf16[2560,512]{1,0:T(8,128)(2,1)S(1)} %multiply_convert_fusion.1) | copy-start | bytes 7864324
  40.0 4.5 %copy-start.1 = (f32[2560,512]{1,0:T(8,128)}, f32[2560,512]{1,0:T(8,128)S(1)}, u32[]{:S(2)}) copy-start(f32[2560,512]{1,0:T(8,128)S(1)} %get-tuple-element.14) | copy-start | bytes 15728644
  41.0 3.5 %copy-start.12 = (f32[2560]{0:T(1024)}, f32[2560]{0:T(1024)S(1)}, u32[]{:S(2)}) copy-start(f32[2560]{0:T(1024)S(1)} %add_sqrt_fusion) | copy-start | bytes 30724
  44.4 18.0 %copy-start.10 = (bf16[64,512]{1,0:T(8,128)(2,1)S(1)}, bf16[64,512]{1,0:T(8,128)(2,1)}, u32[]{:S(2)}) copy-start(bf16[64,512]{1,0:T(8,128)(2,1)} %param.21) | copy-start | bytes 196612
  62.5 3.2 %copy-start.17 = (s32[6,64]{1,0:T(8,128)}, s32[6,64]{1,0:T(8,128)S(1)}, u32[]{:S(2)}) copy-start(s32[6,64]{1,0:T(8,128)S(1)} %subtract_bitcast_fusion) | copy-start | bytes 4612
  83.6 4.0 %copy-start.8 = (bf16[512,512]{1,0:T(8,128)(2,1)S(1)}, bf16[512,512]{1,0:T(8,128)(2,1)}, u32[]{:S(2)}) copy-start(bf16[512,512]{1,0:T(8,128)(2,1)} %param.16) | copy-start | bytes 1572868
  87.6 3.2 %copy-start.15 = (s32[2560]{0:T(1024)S(1)}, s32[2560]{0:T(1024)}, u32[]{:S(2)}) copy-start(s32[2560]{0:T(1024)} %copy-done.14) | copy-start | bytes 30724
  87.6 13.6 %slice-start = ((s8[6291456]{0:T(1024)(128)(4,1)}), s8[4194304]{0:T(1024)(128)(4,1)S(1)}, s32[]{:S(2)}) async-start(s8[6291456]{0:T(1024)(128)(4,1)} %bitcast.96), calls=%async_computation | async-start | bytes 8388608
  90.9 10.4 %slice-start.1 = ((s8[6291456]{0:T(1024)(128)(4,1)}), s8[2097152]{0:T(1024)(128)(4,1)S(1)}, s32[]{:S(2)}) async-start(s8[6291456]{0:T(1024)(128)(4,1)} %bitcast.96), calls=%async_computation.1 | async-start | bytes 4194304
  101.3 3.3 %copy-start.9 = (bf16[227,512]{1,0:T(8,128)(2,1)S(1)}, bf16[227,512]{1,0:T(8,128)(2,1)}, u32[]{:S(2)}) copy-start(bf16[227,512]{1,0:T(8,128)(2,1)} %param.13) | copy-start | bytes 697348
  101.3 5.5 %copy-start.4 = (bf16[2560,512]{1,0:T(8,128)(2,1)S(1)}, bf16[2560,512]{1,0:T(8,128)(2,1)}, u32[]{:S(2)}) copy-start(bf16[2560,512]{1,0:T(8,128)(2,1)} %copy-done.3) | copy-start | bytes 7864324
  106.8 2.3 %copy-start.6 = (bf16[3072,512]{1,0:T(8,128)(2,1)S(1)}, bf16[3072,512]{1,0:T(8,128)(2,1)}, u32[]{:S(2)}) copy-start(bf16[3072,512]{1,0:T(8,128)(2,1)} %copy-done.5) | copy-start | bytes 9437188
  111.7 41.5 %copy-start.13 = (f32[64,512]{1,0:T(8,128)S(1)}, f32[64,512]{1,0:T(8,128)}, u32[]{:S(2)}) copy-start(f32[64,512]{1,0:T(8,128)} %get-tuple-element.11) | copy-start | bytes 393220

commit v3 on v2

--- a/solution.py
+++ b/solution.py
@@ -17,12 +17,6 @@
 def silu_slope(value):
     sigma = jax.nn.sigmoid(value)
     return sigma * (1.0 + value * (1.0 - sigma))
-
-
-def normalize(value):
-    centred = value - jnp.mean(value, axis=-1, keepdims=True)
-    spread = jnp.sqrt(jnp.mean(centred * centred, axis=-1, keepdims=True) + EPSILON)
-    return (centred / spread, spread)
 
 
 def times_transpose(left, right):
@@ -496,6 +490,83 @@
     return [result.reshape(rows, latent) for result in results[:-1]] + [results[-1]]
 
 
+def encode_kernel(edges, g_ref, d_ref, m_ref, w_ref, a_ref, l_ref, n_ref, i_ref, h_ref):
+    rows, latent = d_ref.shape
+    before = g_ref[...].astype(F32).reshape(rows, edges, latent) + d_ref[...][:, None, :]
+    before = before.reshape(rows * edges, latent)
+    sigma = jax.nn.sigmoid(before)
+    active = before * sigma
+    l_ref[...] = (sigma + active * (1.0 - sigma)).astype(BF16)
+    active = active.astype(BF16)
+    a_ref[...] = active
+    out = jnp.dot(active, w_ref[...], preferred_element_type=F32)
+    out = out - jnp.mean(out, axis=-1, keepdims=True)
+    inverse = 1.0 / jnp.sqrt(jnp.mean(out * out, axis=-1, keepdims=True) + EPSILON)
+    out = out * inverse
+    i_ref[...] = inverse
+    n_ref[...] = out.astype(BF16)
+    encoded = jnp.sum(out.reshape(rows, edges, latent), axis=1)
+    h_ref[...] = (m_ref[...].astype(F32) + encoded * (1.0 / math.sqrt(edges))).astype(BF16)
+
+
+def rows_spec(rows, width):
+    return pl.BlockSpec((rows, width), lambda i: (i, 0))
+
+
+def encode(gathered, dest, mesh_in, w_edge, edges, tile):
+    rows, latent = dest.shape
+    total = rows * edges
+    wide = rows_spec(tile * edges, latent)
+    return pl.pallas_call(
+        functools.partial(encode_kernel, edges),
+        grid=(rows // tile,),
+        out_shape=[jax.ShapeDtypeStruct((total, latent), BF16)] * 3
+        + [
+            jax.ShapeDtypeStruct((total, 1), F32),
+            jax.ShapeDtypeStruct((rows, latent), BF16),
+        ],
+        in_specs=[
+            wide,
+            rows_spec(tile, latent),
+            rows_spec(tile, latent),
+            pl.BlockSpec((latent, latent), lambda i: (0, 0)),
+        ],
+        out_specs=[wide] * 3 + [rows_spec(tile * edges, 1), rows_spec(tile, latent)],
+        name="encode",
+    )(gathered, dest, mesh_in, w_edge)
+
+
+def decode_kernel(edges, u_ref, n_ref, i_ref, l_ref, w_ref, g_ref, b_ref):
+    rows, latent = u_ref.shape
+    upper = u_ref[...] * (1.0 / math.sqrt(edges))
+    normed = n_ref[...].astype(F32).reshape(rows, edges, latent)
+    both = jnp.mean(upper[:, None, :] * normed, axis=-1, keepdims=True)
+    upper = upper - jnp.mean(upper, axis=-1, keepdims=True)
+    grad = (upper[:, None, :] - normed * both).reshape(rows * edges, latent) * i_ref[...]
+    grad = grad.astype(BF16)
+    g_ref[...] = grad
+    b_ref[...] = (times_transpose(grad, w_ref[...]) * l_ref[...].astype(F32)).astype(BF16)
+
+
+def decode(mesh_grad, normed, inverse, slope, w_edge, edges, tile):
+    rows, latent = mesh_grad.shape
+    wide = rows_spec(tile * edges, latent)
+    return pl.pallas_call(
+        functools.partial(decode_kernel, edges),
+        grid=(rows // tile,),
+        out_shape=[jax.ShapeDtypeStruct((rows * edges, latent), BF16)] * 2,
+        in_specs=[
+            rows_spec(tile, latent),
+            wide,
+            rows_spec(tile * edges, 1),
+            wide,
+            pl.BlockSpec((latent, latent), lambda i: (0, 0)),
+        ],
+        out_specs=[wide] * 2,
+        name="decode",
+    )(mesh_grad, normed, inverse, slope, w_edge)
+
+
 def one_hot(index, count):
     return (index[:, None] == lax.broadcasted_iota(jnp.int32, (1, count), 1)).astype(BF16)
 
@@ -519,14 +590,10 @@
     projected = jnp.dot(hidden, w_src, preferred_element_type=F32).astype(BF16)
     dest_term = jnp.dot(mesh_in, w_dst, preferred_element_type=F32)
     grid_local = (g2m_src - (band_index * (nodes * subs) - nodes)).reshape(-1)
-    before = jnp.take(projected, grid_local, axis=0).astype(F32)
-    before = (before.reshape(mesh_rows, enc_count, latent) + dest_term[:, None, :]).reshape(
-        -1, latent
+    gathered = jnp.take(projected, grid_local, axis=0)
+    active, slope, normed, inverse, hidden_mesh = encode(
+        gathered, dest_term, mesh_in, w_edge, enc_count, 16
     )
-    active = jax.nn.silu(before).astype(BF16)
-    normed, spread = normalize(jnp.dot(active, w_edge, preferred_element_type=F32))
-    encoded = jnp.sum(normed.reshape(mesh_rows, enc_count, latent), axis=1)
-    hidden_mesh = (mesh_in.astype(F32) + encoded / math.sqrt(enc_count)).astype(BF16)
     query = jnp.dot(hidden_mesh, w_proc, preferred_element_type=F32).astype(BF16)
     receiver = jnp.dot(hidden_mesh, w_recv, preferred_element_type=F32)
     mesh_window = fetch_window(query, bands, subs, 1).reshape(slots * mesh_rows, latent)
@@ -543,15 +610,8 @@
     query_grad = return_window(query_window.reshape(slots, mesh_rows, latent), bands, subs, 2)
     mesh_grad = upstream + times_transpose(query_grad.astype(BF16), w_proc)
     mesh_grad = mesh_grad + times_transpose(receiver_grad.astype(BF16), w_recv)
-    upper = mesh_grad / math.sqrt(enc_count)
-    incoming = jnp.broadcast_to(upper[:, None, :], (mesh_rows, enc_count, latent)).reshape(
-        -1, latent
-    )
-    centred_grad = incoming - jnp.mean(incoming, axis=-1, keepdims=True)
-    centred_grad = centred_grad - normed * jnp.mean(incoming * normed, axis=-1, keepdims=True)
-    norm_grad = (centred_grad / spread).astype(BF16)
+    norm_grad, before_grad = decode(mesh_grad, normed, inverse, slope, w_edge, enc_count, 16)
     edge_part = first_contract(active, norm_grad)
-    before_grad = (times_transpose(norm_grad, w_edge) * silu_slope(before)).astype(BF16)
     window_grad = first_contract(one_hot(grid_local, slots * nodes), before_grad).astype(BF16)
     src_part = first_contract(hidden, window_grad)
     hidden_grad = (times_transpose(window_grad, w_src) * silu_slope(hidden_pre)).astype(BF16)

time: 156 us -> 150 us (0.962)
  Pallas kernels: 72.2 us -> 86.5 us
  other arithmetic: 23.8 us -> 10 us
  matrix products: 44.9 us -> 38.1 us
    pallas_call x0 -> x2, Pallas kernels: none -> 14.1 us  [the longest x1 7.3 us: decode(): pl.pallas_call(functools.partial(decode_kernel, edges), grid=(rows // til...]
    reduce_sum x3 -> x0, other arithmetic: 7.96 us -> none  [the longest x1 3.62 us: body(): jnp.mean(incoming * normed, axis=-1, keepdims=True)]
    convert_element_type x3 -> x0, other arithmetic: 6.41 us -> none  [the longest x1 3.98 us: body(): norm_grad = (centred_grad / spread).astype(BF16)]
    dot_general x4 -> x3, matrix products: 9.34 us -> 5.39 us  [times_transpose(): lax.dot_general(left, right, (((1,), (1,)), ((), ())), preferred_element_...]
    div x4 -> x0, other arithmetic: 3.47 us -> none  [the longest x1 3.45 us: normalize(): return (centred / spread, spread)]
    select_n x1 -> x2, other arithmetic: 0.04 us -> 2.47 us  [body(): gathered = jnp.take(projected, grid_local, axis=0)]
    dot_general x1 -> x0, matrix products: 1.59 us -> none  [body(): jnp.dot(active, w_edge, preferred_element_type=F32)]
    unnamed x41 -> x29, local copies, waits for them, and re-layouts: 2.51 us -> 3.46 us
where the time goes in v3:
time: 150 us; the launch traced here: 149 us
  Pallas kernels  86.5 us (58%)
  matrix products  38.1 us (25%)
  local copies, waits for them, and re-layouts  13.8 us (9%)
  other arithmetic  10 us (7%)
    pallas_call x1, Pallas kernels, tail(): pl.pallas_call(functools.partial(tail_kernel, bands, subs, len(values)),...  38.6 us
    pallas_call x2, Pallas kernels, fetch_window(): pl.pallas_call(functools.partial(window_kernel, bands, subs), out_shape=j...  25.3 us
    dot_general x4, matrix products, first_contract(): lax.dot_general(left, right, (((0,), (0,)), ((), ())), preferred_element_...  18.2 us
    gather x1, local copies, waits for them, and re-layouts, body(): gathered = jnp.take(projected, grid_local, axis=0)  10 us
    pallas_call x1, Pallas kernels, return_window(): pl.pallas_call(functools.partial(return_kernel, bands, subs), out_shape=j...  8.47 us
    pallas_call x1, Pallas kernels, decode(): pl.pallas_call(functools.partial(decode_kernel, edges), grid=(rows // til...  7.3 us
    pallas_call x1, Pallas kernels, encode(): pl.pallas_call(functools.partial(encode_kernel, edges), grid=(rows // til...  6.77 us
    dot_general x3, matrix products, times_transpose(): lax.dot_general(left, right, (((1,), (1,)), ((), ())), preferred_element_...  5.39 us

profile of v3, /device:TPU:13, one launch (start us, length us, event | category | flops | bytes accessed | tf_op | source)
XLA Modules:
  0.0 149.3 jit_solution(17245446027638863926)
XLA Ops:
  0.6 0.0 copy-start
  0.7 0.7 subtract_bitcast_fusion
  1.4 0.1 eq.57
  1.5 0.7 broadcast_subtract_fusion
  2.2 0.1 copy.15
  2.3 0.1 reshape.104
  2.4 0.1 reshape.102
  2.6 1.9 %fusion.24.d_ref = f32[64,512]{1,0:T(8,128)} fusion(bf16[64,512]{1,0:T(8,128)(2,1)} %m_ref.1, bf16[512,512]{1,0:T(8,128)(2,1)} %param.15), kind=kOutput, calls=%fused_computation.53 | convolution fusion | flops 33554432 | bytes 720896 | tf_op jit(solution)/shard_map/dot_general | solution.py:591
  4.5 0.9 convert_multiply_fusion
  5.4 16.0 %window0.1 = bf16[6,227,512]{2,1,0:T(8,128)(2,1)} custom-call(bf16[227,512]{1,0:T(8,128)(2,1)} %x_ref.1), custom_call_target="tpu_custom_call" | custom-call | tf_op jit(solution)/shard_map/window0/pallas_call | solution.py:180
  21.3 2.5 %fusion.17 = f32[6,512,512]{2,1,0:T(8,128)S(1)} fusion(bf16[6,227,512]{2,1,0:T(8,128)(2,1)} %window0.1, bf16[227,512]{1,0:T(8,128)(2,1)} %param.13), kind=kOutput, calls=%fused_computation.38 | convolution fusion | flops 714080256 | bytes 7918592 | tf_op jit(solution)/shard_map/dot_general | solution.py:586
  23.8 0.0 copy-start.1
  23.8 1.7 %fusion.5 = bf16[3072,512]{1,0:T(8,128)(2,1)S(1)} fusion(f32[6,512,512]{2,1,0:T(8,128)S(1)} %fusion.17), kind=kLoop, calls=%fused_computation.10 | loop fusion | flops 7864320 | bytes 9437184 | tf_op jit(solution)/shard_map/convert_element_type | solution.py:589
  25.6 0.9 copy-done.1
  26.5 1.7 %copy-done.2 = bf16[3072,512]{1,0:T(8,128)(2,1)} copy-done((bf16[3072,512]{1,0:T(8,128)(2,1)}, bf16[3072,512]{1,0:T(8,128)(2,1)S(1)}, u32[]{:S(2)}) %copy-start.2) | copy-done | bytes 3145752
  28.2 0.0 copy-done
  28.2 3.4 %convolution_convert_fusion = bf16[3072,512]{1,0:T(8,128)(2,1)} fusion(bf16[3072,512]{1,0:T(8,128)(2,1)S(1)} %fusion.5, bf16[512,512]{1,0:T(8,128)(2,1)S(1)} %copy-done), kind=kOutput, calls=%fused_computation.16 | convolution fusion | flops 1612185600 | bytes 6815744 | tf_op jit(solution)/shard_map/dot_general | solution.py:590
  31.6 10.0 %gather_fusion = bf16[2560,512]{1,0:T(8,128)(2,1)S(1)} fusion(bf16[3072,512]{1,0:T(8,128)(2,1)} %convolution_convert_fusion, s32[3072]{0:T(1024)S(1)} %pad_clamp_fusion), kind=kCustom, calls=%fused_computation | custom fusion | bytes 5253120 | tf_op jit(solution)/shard_map/jit(_take)/gather | solution.py:593
  41.7 2.4 %broadcast_select_fusion.g_ref = bf16[2560,512]{1,0:T(8,128)(2,1)} fusion(bf16[2560,512]{1,0:T(8,128)(2,1)S(1)} %gather_fusion, pred[2560]{0:T(1024)(128)(4,1)S(1)} %compare_and_fusion), kind=kLoop, calls=%fused_computation.17 | loop fusion | flops 1310720 | bytes 5245440 | tf_op jit(solution)/shard_map/jit(_take)/select_n | solution.py:593
  44.1 6.8 %encode.1 = (bf16[2560,512]{1,0:T(8,128)(2,1)}, bf16[2560,512]{1,0:T(8,128)(2,1)}, bf16[2560,512]{1,0:T(8,128)(2,1)}, f32[2560,1]{1,0:T(8,128)}, bf16[64,512]{1,0:T(8,128)(2,1)}) custom-call(bf16[2560,512]{1,0:T(8,128)(2,1)} %broadcast_select_fusion.g_ref, f32[64,512]{1,0:T(8,128)} %fusion.24.d_ref, bf16[64,512]{1,0:T(8,128)(2,1)} %m_ref.1, ...), custom_call_target="tpu_custom_call" | custom-call | tf_op jit(solution)/shard_map/encode/pallas_call | solution.py:520
  50.9 0.0 copy-done.4
  50.9 1.7 %convolution_convert_fusion.5.x_ref = bf16[64,512]{1,0:T(8,128)(2,1)} fusion(bf16[64,512]{1,0:T(8,128)(2,1)} %get-tuple-element.14, bf16[512,512]{1,0:T(8,128)(2,1)S(1)} %copy-done.4), kind=kOutput, calls=%fused_computation.26 | convolution fusion | flops 33587200 | bytes 655360 | tf_op jit(solution)/shard_map/dot_general | solution.py:597
  52.6 0.0 copy-done.5
  52.6 1.0 fusion.25
  53.6 0.0 copy-start.7
  53.6 9.3 %window1.1 = bf16[6,64,512]{2,1,0:T(8,128)(2,1)} custom-call(bf16[64,512]{1,0:T(8,128)(2,1)} %convolution_convert_fusion.5.x_ref), custom_call_target="tpu_custom_call" | custom-call | tf_op jit(solution)/shard_map/window1/pallas_call | solution.py:180
  62.9 0.0 copy-start.9
  62.9 1.8 %fusion.22 = (bf16[64,512]{1,0:T(8,128)(2,1)S(1)}, f32[64,512]{1,0:T(8,128)S(1)}, bf16[6,64,512]{2,1,0:T(8,128)(2,1)S(1)}) fusion(f32[64,512]{1,0:T(8,128)S(1)} %convert_multiply_fusion, f32[64,512]{1,0:T(8,128)S(1)} %fusion.25, bf16[384,512,1]{1,0,2:T(8,128)(2,1)} %bitcast.79, s32[6,64]{1,0:T(8,128)S(1)} %subtract_bitcast_fusion), kind=kOutput, calls=%fused_computation.51 | convolution fusion | flops 153632768 | bytes 1246720 | tf_op jit(solution)/shard_map/dot_general | solution.py:602
  64.7 0.0 copy-done.7
  64.7 0.6 add_convert_fusion
  65.4 1.2 convolution_convert_fusion.4
  66.6 8.5 %return2.1 = f32[64,512]{1,0:T(8,128)} custom-call(bf16[6,64,512]{2,1,0:T(8,128)(2,1)} %bitcast.80), custom_call_target="tpu_custom_call" | custom-call | tf_op jit(solution)/shard_map/return2/pallas_call | solution.py:315
  75.1 1.2 convolution_add_fusion.2
  76.3 0.9 convolution_add_fusion.1.u_ref
  77.2 7.3 %decode.1 = (bf16[2560,512]{1,0:T(8,128)(2,1)}, bf16[2560,512]{1,0:T(8,128)(2,1)}) custom-call(f32[64,512]{1,0:T(8,128)} %convolution_add_fusion.1.u_ref, bf16[2560,512]{1,0:T(8,128)(2,1)} %get-tuple-element.15.n_ref, f32[2560,1]{1,0:T(8,128)} %get-tuple-element.16.i_ref, bf16[2560,512]{1,0:T(8,128)(2,1)} %get-tuple-element.17.l_ref, bf16[512,512]{1,0:T(8,128)(2,1)} %w_ref.3), custom_call_target="tpu_custom_call" | custom-call | tf_op jit(solution)/shard_map/decode/pallas_call | solution.py:554
  84.5 0.0 copy-done.10
  84.5 0.0 slice-start
  84.5 4.2 %convolution_convert_fusion.3 = bf16[512,512]{1,0:T(8,128)(2,1)} fusion(bf16[2560,512]{1,0:T(8,128)(2,1)S(1)} %copy-done.10, bf16[2560,512]{1,0:T(8,128)(2,1)} %get-tuple-element.20), kind=kOutput, calls=%fused_computation.21 | convolution fusion | flops 1342439424 | bytes 5767168 | tf_op jit(solution)/shard_map/dot_general | solution.py:27
  88.8 10.1 %fusion.10 = bf16[3072,512]{1,0:T(8,128)(2,1)S(1)} fusion(bf16[2560,512]{1,0:T(8,128)(2,1)S(1)} %copy-done.11, s32[2560]{0:T(1024)S(1)} %reshape.102), kind=kOutput, calls=%fused_computation.15 | convolution fusion | flops 8062500864 | bytes 5777408 | tf_op jit(solution)/shard_map/dot_general | solution.py:27
  98.9 0.0 slice-done
  98.9 0.0 slice-done.1
  98.9 3.3 %fusion.9 = bf16[3072,512]{1,0:T(8,128)(2,1)S(1)} fusion(f32[6,512,512]{2,1,0:T(8,128)S(1)} %bitcast.75, bf16[3072,512]{1,0:T(8,128)(2,1)S(1)} %fusion.10, bf16[512,512]{1,0:T(8,128)(2,1)S(1)} %copy-done), kind=kOutput, calls=%fused_computation.14 | convolution fusion | flops 1624768512 | bytes 13107200 | tf_op jit(solution)/shard_map/dot_general | solution.py:23
  102.2 0.0 copy-start.6
  102.2 2.6 %convolution_convert_fusion.2 = bf16[512,512]{1,0:T(8,128)(2,1)} fusion(bf16[3072,512]{1,0:T(8,128)(2,1)S(1)} %copy-done.3, bf16[3072,512]{1,0:T(8,128)(2,1)S(1)} %fusion.10), kind=kOutput, calls=%fused_computation.20 | convolution fusion | flops 1610874880 | bytes 6815744 | tf_op jit(solution)/shard_map/dot_general | solution.py:27
  104.8 2.2 %fusion.11.refs_2_ = bf16[6,227,512]{2,1,0:T(8,128)(2,1)} fusion(bf16[6,512,512]{2,1,0:T(8,128)(2,1)S(1)} %bitcast.76, bf16[227,512]{1,0:T(8,128)(2,1)S(1)} %copy-done.6), kind=kOutput, calls=%fused_computation.19 | convolution fusion | flops 714777600 | bytes 4772864 | tf_op jit(solution)/shard_map/dot_general | solution.py:618
  107.0 38.6 %tail.1 = (bf16[32,16,512]{2,1,0:T(8,128)(2,1)}, bf16[32,16,512]{2,1,0:T(8,128)(2,1)}, f32[227,512]{1,0:T(8,128)}) custom-call(bf16[32,16,512]{2,1,0:T(8,128)(2,1)} %bitcast.78, bf16[32,16,512]{2,1,0:T(8,128)(2,1)} %bitcast.77, bf16[6,227,512]{2,1,0:T(8,128)(2,1)} %fusion.11.refs_2_), custom_call_target="tpu_custom_call" | custom-call | tf_op jit(solution)/shard_map/tail/pallas_call | solution.py:480
  145.7 2.9 %bitcast_convert_fusion = (f32[512,512]{1,0:T(8,128)}, f32[512,512]{1,0:T(8,128)}) fusion(bf16[32,16,512]{2,1,0:T(8,128)(2,1)} %get-tuple-element.23, bf16[32,16,512]{2,1,0:T(8,128)(2,1)} %get-tuple-element.22), kind=kLoop, calls=%fused_computation.33 | loop fusion | flops 524288 | bytes 3145728 | tf_op jit(solution)/shard_map/convert_element_type | solution.py:628
  148.5 0.8 copy.18
  (17 shorter events, 0.1 us)
Async XLA Ops:
  0.6 27.6 %copy-start = (bf16[512,512]{1,0:T(8,128)(2,1)S(1)}, bf16[512,512]{1,0:T(8,128)(2,1)}, u32[]{:S(2)}) copy-start(bf16[512,512]{1,0:T(8,128)(2,1)} %param.14) | copy-start | bytes 1572868
  23.8 2.7 %copy-start.1 = (f32[6,512,512]{2,1,0:T(8,128)}, f32[6,512,512]{2,1,0:T(8,128)S(1)}, u32[]{:S(2)}) copy-start(f32[6,512,512]{2,1,0:T(8,128)S(1)} %fusion.17) | copy-start | bytes 18874372
  26.5 1.7 %copy-start.2 = (bf16[3072,512]{1,0:T(8,128)(2,1)}, bf16[3072,512]{1,0:T(8,128)(2,1)S(1)}, u32[]{:S(2)}) copy-start(bf16[3072,512]{1,0:T(8,128)(2,1)S(1)} %fusion.5) | copy-start | bytes 9437188
  44.1 6.8 %copy-start.4 = (bf16[512,512]{1,0:T(8,128)(2,1)S(1)}, bf16[512,512]{1,0:T(8,128)(2,1)}, u32[]{:S(2)}) copy-start(bf16[512,512]{1,0:T(8,128)(2,1)} %param.17) | copy-start | bytes 1572868
  44.1 8.5 %copy-start.5 = (bf16[512,512]{1,0:T(8,128)(2,1)S(1)}, bf16[512,512]{1,0:T(8,128)(2,1)}, u32[]{:S(2)}) copy-start(bf16[512,512]{1,0:T(8,128)(2,1)} %param.18) | copy-start | bytes 1572868
  53.6 11.1 %copy-start.7 = (bf16[64,512]{1,0:T(8,128)(2,1)S(1)}, bf16[64,512]{1,0:T(8,128)(2,1)}, u32[]{:S(2)}) copy-start(bf16[64,512]{1,0:T(8,128)(2,1)} %get-tuple-element.14) | copy-start | bytes 196612
  62.9 12.2 %copy-start.9 = (bf16[64,512]{1,0:T(8,128)(2,1)S(1)}, bf16[64,512]{1,0:T(8,128)(2,1)}, u32[]{:S(2)}) copy-start(bf16[64,512]{1,0:T(8,128)(2,1)} %param.21) | copy-start | bytes 196612
  77.2 7.3 %copy-start.10 = (bf16[2560,512]{1,0:T(8,128)(2,1)S(1)}, bf16[2560,512]{1,0:T(8,128)(2,1)}, u32[]{:S(2)}) copy-start(bf16[2560,512]{1,0:T(8,128)(2,1)} %get-tuple-element.19) | copy-start | bytes 7864324
  84.5 4.2 %copy-start.11 = (bf16[2560,512]{1,0:T(8,128)(2,1)S(1)}, bf16[2560,512]{1,0:T(8,128)(2,1)}, u32[]{:S(2)}) copy-start(bf16[2560,512]{1,0:T(8,128)(2,1)} %get-tuple-element.18) | copy-start | bytes 7864324
  84.5 14.4 %slice-start = ((s8[6291456]{0:T(1024)(128)(4,1)}), s8[4194304]{0:T(1024)(128)(4,1)S(1)}, s32[]{:S(2)}) async-start(s8[6291456]{0:T(1024)(128)(4,1)} %bitcast.74), calls=%async_computation | async-start | bytes 8388608
  88.8 10.1 %slice-start.1 = ((s8[6291456]{0:T(1024)(128)(4,1)}), s8[2097152]{0:T(1024)(128)(4,1)S(1)}, s32[]{:S(2)}) async-start(s8[6291456]{0:T(1024)(128)(4,1)} %bitcast.74), calls=%async_computation.1 | async-start | bytes 4194304
  98.9 3.3 %copy-start.3 = (bf16[3072,512]{1,0:T(8,128)(2,1)S(1)}, bf16[3072,512]{1,0:T(8,128)(2,1)}, u32[]{:S(2)}) copy-start(bf16[3072,512]{1,0:T(8,128)(2,1)} %copy-done.2) | copy-start | bytes 9437188
  102.2 2.6 %copy-start.6 = (bf16[227,512]{1,0:T(8,128)(2,1)S(1)}, bf16[227,512]{1,0:T(8,128)(2,1)}, u32[]{:S(2)}) copy-start(bf16[227,512]{1,0:T(8,128)(2,1)} %param.13) | copy-start | bytes 697348
  145.6 2.9 %copy-start.8 = (f32[227,512]{1,0:T(8,128)S(1)}, f32[227,512]{1,0:T(8,128)}, u32[]{:S(2)}) copy-start(f32[227,512]{1,0:T(8,128)} %get-tuple-element.34) | copy-start | bytes 1394692

commit v4 on v3

--- a/solution.py
+++ b/solution.py
@@ -193,7 +193,7 @@
 
 
 def return_stream(
-    bands, subs, g_ref, o_ref, pairbuf, stage, far, edge, send1, recv1, send2, far_sem, edge_sem
+    bands, subs, work, g_ref, o_ref, pairbuf, stage, far, edge, send1, recv1, send2, far_sem, edge_sem
 ):
     band, me, core, chip, partner, chips = place(subs)
     order = list(range(1, chips)) + [chips, 0]
@@ -205,6 +205,7 @@
 
     swaps = {}
     for step in order:
+        work(slot_of(step, 1 - core))
         swaps[step] = remote(
             g_ref.at[slot_of(step, 1 - core)],
             pairbuf.at[step],
@@ -213,9 +214,10 @@
             (band, partner),
         )
         swaps[step].start()
-    yield
+        yield
 
     def combined(step):
+        work(slot_of(step, core))
         swaps[step].wait_recv()
         return g_ref[slot_of(step, core)].astype(F32) + pairbuf[step].astype(F32)
 
@@ -231,6 +233,7 @@
         )
         copy.start()
         across.append(copy)
+        yield
     stage[chips - 1] = combined(chips).astype(BF16)
 
     def border(b, s):
@@ -251,6 +254,7 @@
 
     yield
     total = combined(0)
+    yield
     for step, copy in enumerate(across):
         copy.wait_recv()
         total = total + far[step].astype(F32)
@@ -290,7 +294,7 @@
 def return_kernel(bands, subs, *refs):
     band, me = (lax.axis_index("band"), lax.axis_index("sub"))
     near_barrier(bands, subs, band, me)
-    for _ in return_stream(bands, subs, *refs):
+    for _ in return_stream(bands, subs, lambda slot: None, *refs):
         pass
 
 
@@ -431,7 +435,7 @@
     )
 
 
-def tail_kernel(bands, subs, streams, *refs):
+def tail_kernel(bands, subs, *refs):
     band, me = (lax.axis_index("band"), lax.axis_index("sub"))
     barrier = pltpu.get_barrier_semaphore()
     for step in range(1, subs):
@@ -456,38 +460,60 @@
 
     sides = jnp.minimum(band, 1) + jnp.minimum(bands - 1 - band, 1)
     pl.semaphore_wait(barrier, subs + bands - 2 + (subs - 1) * sides)
-    count = streams + 1
-    ins, outs, scratch = (refs[:count], refs[count : 2 * count], refs[2 * count :])
-    active = [
-        sum_stream(bands, subs, ins[i], outs[i], *scratch[17 * i : 17 * i + 17])
-        for i in range(streams)
-    ]
-    active.append(return_stream(bands, subs, ins[-1], outs[-1], *scratch[17 * streams :]))
+    v_ref, index_ref, b_ref, hidden_ref, slope_ref, src_ref, embed_ref = refs[:7]
+    src_out, edge_out, grid_out, slots, parts, total = refs[7:13]
+    scratch = refs[13:]
+    nodes = hidden_ref.shape[1]
+    edges = index_ref.shape[1]
+    total[...] = jnp.zeros_like(total)
+
+    def work(slot):
+        rows = lax.broadcasted_iota(jnp.int32, (nodes, edges), 0)
+        picks = jnp.where(rows == index_ref[...] - slot * nodes, 1.0, 0.0).astype(BF16)
+        grad = jnp.dot(picks, b_ref[...], preferred_element_type=F32).astype(BF16)
+        total[...] += first_contract(hidden_ref[slot], grad)
+        grad = times_transpose(grad, src_ref[...]) * slope_ref[slot].astype(F32)
+        slots[slot] = times_transpose(embed_ref[...], grad.astype(BF16)).astype(BF16)
+
+    edge = sum_stream(bands, subs, v_ref, edge_out, *scratch[:17])
+    src = sum_stream(bands, subs, parts, src_out, *scratch[17:34])
+    back = return_stream(bands, subs, work, slots, grid_out, *scratch[34:])
+    next(edge)
+    for _ in range(subs + 2):
+        next(back)
+        next(edge, True)
+    deep = parts.shape[1]
+    for i in range(parts.shape[0]):
+        parts[i] = total[i * deep : (i + 1) * deep].astype(BF16)
+    active = [src, back, edge]
     while active:
         active = [stream for stream in active if next(stream, True) is None]
 
 
-def tail(values, slots, bands, subs, ident):
+def tail(edge_part, index, before_grad, hidden, slope, w_src, w_embed, bands, subs, ident):
     chips = subs // 2
     count = bands * subs
-    rows, latent = values[0].shape
-    deep = rows // count
-    block = slots.shape[1:]
+    latent = w_src.shape[0]
+    slots, nodes, _ = hidden.shape
+    block = (w_embed.shape[0], nodes)
+    deep = latent // count
     shape = (count, deep, latent)
-    scratch = []
-    for _ in values:
-        scratch += sum_scratch(chips, bands, deep, latent)
-    results = pl.pallas_call(
-        functools.partial(tail_kernel, bands, subs, len(values)),
-        out_shape=[jax.ShapeDtypeStruct(shape, BF16)] * len(values)
-        + [jax.ShapeDtypeStruct(block, F32)],
-        in_specs=[VMEM] * (len(values) + 1),
-        out_specs=[VMEM] * (len(values) + 1),
-        scratch_shapes=scratch + return_scratch(chips, block),
+    src, edge, grid = pl.pallas_call(
+        functools.partial(tail_kernel, bands, subs),
+        out_shape=[jax.ShapeDtypeStruct(shape, BF16)] * 2 + [jax.ShapeDtypeStruct(block, F32)],
+        in_specs=[VMEM] * 7,
+        out_specs=[VMEM] * 3,
+        scratch_shapes=[
+            pltpu.VMEM((slots,) + block, BF16),
+            pltpu.VMEM(shape, BF16),
+            pltpu.VMEM((latent, latent), F32),
+        ]
+        + sum_scratch(chips, bands, deep, latent) * 2
+        + return_scratch(chips, block),
         compiler_params=pltpu.CompilerParams(collective_id=ident, has_side_effects=True),
         name="tail",
-    )(*[value.reshape(shape) for value in values], slots)
-    return [result.reshape(rows, latent) for result in results[:-1]] + [results[-1]]
+    )(edge_part.reshape(shape), index, before_grad, hidden, slope, w_src, w_embed)
+    return src.reshape(latent, latent), edge.reshape(latent, latent), grid
 
 
 def encode_kernel(edges, g_ref, d_ref, m_ref, w_ref, a_ref, l_ref, n_ref, i_ref, h_ref):
@@ -590,7 +616,7 @@
     projected = jnp.dot(hidden, w_src, preferred_element_type=F32).astype(BF16)
     dest_term = jnp.dot(mesh_in, w_dst, preferred_element_type=F32)
     grid_local = (g2m_src - (band_index * (nodes * subs) - nodes)).reshape(-1)
-    gathered = jnp.take(projected, grid_local, axis=0)
+    gathered = projected.at[grid_local].get(mode="promise_in_bounds")
     active, slope, normed, inverse, hidden_mesh = encode(
         gathered, dest_term, mesh_in, w_edge, enc_count, 16
     )
@@ -612,18 +638,17 @@
     mesh_grad = mesh_grad + times_transpose(receiver_grad.astype(BF16), w_recv)
     norm_grad, before_grad = decode(mesh_grad, normed, inverse, slope, w_edge, enc_count, 16)
     edge_part = first_contract(active, norm_grad)
-    window_grad = first_contract(one_hot(grid_local, slots * nodes), before_grad).astype(BF16)
-    src_part = first_contract(hidden, window_grad)
-    hidden_grad = (times_transpose(window_grad, w_src) * silu_slope(hidden_pre)).astype(BF16)
-    grid_part = lax.dot_general(
+    src_grad, edge_grad, grid_grad = tail(
+        edge_part.astype(BF16),
+        grid_local[None, :],
+        before_grad,
+        hidden.reshape(slots, nodes, latent),
+        silu_slope(hidden_pre).astype(BF16).reshape(slots, nodes, latent),
+        w_src,
         w_embed,
-        hidden_grad.reshape(slots, nodes, latent),
-        (((1,), (2,)), ((), ())),
-        preferred_element_type=F32,
-    )
-    grid_part = jnp.swapaxes(grid_part, 0, 1).astype(BF16)
-    src_grad, edge_grad, grid_grad = tail(
-        [src_part.astype(BF16), edge_part.astype(BF16)], grid_part, bands, subs, 3
+        bands,
+        subs,
+        3,
     )
     return (mesh_out, grid_grad, src_grad.astype(F32), edge_grad.astype(F32))
 

time: 150 us -> 152 us (1.013)
  Pallas kernels: 86.5 us -> 105 us
  matrix products: 38.1 us -> 24.5 us
  other arithmetic: 10 us -> 7.6 us
    pallas_call x1, Pallas kernels: 38.6 us -> 57 us  [tail(): pl.pallas_call(functools.partial(tail_kernel, bands, subs), out_shape=[ja...]
    dot_general x4 -> x2, matrix products: 18.2 us -> 5.31 us  [first_contract(): lax.dot_general(left, right, (((0,), (0,)), ((), ())), preferred_element_...]
    dot_general x1, matrix products: 2.48 us -> 7.16 us  [body(): lax.dot_general(x_window, w_embed, (((1,), (0,)), ((), ())), preferred_el...]
    dot_general x3 -> x2, matrix products: 5.39 us -> 2.13 us  [times_transpose(): lax.dot_general(left, right, (((1,), (1,)), ((), ())), preferred_element_...]
    unnamed x29 -> x15, local copies, waits for them, and re-layouts: 3.46 us -> 0.81 us
    select_n x2 -> x1, other arithmetic: 2.47 us -> 0.04 us  [body(): gathered = projected.at[grid_local].get(mode='promise_in_bounds')]
    dot_general x1 -> x0, matrix products: 2.16 us -> none  [body(): lax.dot_general(w_embed, hidden_grad.reshape(slots, nodes, latent), (((1,...]
where the time goes in v4:
time: 152 us; the launch traced here: 150 us
  Pallas kernels  105 us (69%)
  matrix products  24.5 us (16%)
  local copies, waits for them, and re-layouts  12.4 us (8%)
  other arithmetic  7.6 us (5%)
    pallas_call x1, Pallas kernels, tail(): pl.pallas_call(functools.partial(tail_kernel, bands, subs), out_shape=[ja...  57 us
    pallas_call x2, Pallas kernels, fetch_window(): pl.pallas_call(functools.partial(window_kernel, bands, subs), out_shape=j...  25.3 us
    gather x1, local copies, waits for them, and re-layouts, body(): gathered = projected.at[grid_local].get(mode='promise_in_bounds')  10.6 us
    pallas_call x1, Pallas kernels, return_window(): pl.pallas_call(functools.partial(return_kernel, bands, subs), out_shape=j...  8.47 us
    pallas_call x1, Pallas kernels, decode(): pl.pallas_call(functools.partial(decode_kernel, edges), grid=(rows // til...  7.27 us
    dot_general x1, matrix products, body(): lax.dot_general(x_window, w_embed, (((1,), (0,)), ((), ())), preferred_el...  7.16 us
    pallas_call x1, Pallas kernels, encode(): pl.pallas_call(functools.partial(encode_kernel, edges), grid=(rows // til...  6.71 us
    dot_general x2, matrix products, first_contract(): lax.dot_general(left, right, (((0,), (0,)), ((), ())), preferred_element_...  5.31 us

profile of v4, /device:TPU:13, one launch (start us, length us, event | category | flops | bytes accessed | tf_op | source)
XLA Modules:
  0.0 150.1 jit_solution(1399205063094467410)
XLA Ops:
  0.6 0.0 copy-start
  0.7 0.7 subtract_bitcast_fusion
  1.4 0.1 eq.41
  1.5 0.7 broadcast_subtract_fusion
  2.2 0.1 copy.16
  2.3 0.7 broadcast_in_dim_reshape.4.refs_1_
  3.0 0.1 reshape.90
  3.1 1.9 %fusion.15.d_ref = f32[64,512]{1,0:T(8,128)} fusion(bf16[64,512]{1,0:T(8,128)(2,1)} %m_ref.1, bf16[512,512]{1,0:T(8,128)(2,1)} %param.15), kind=kOutput, calls=%fused_computation.40 | convolution fusion | flops 33554432 | bytes 720896 | tf_op jit(solution)/shard_map/dot_general | solution.py:617
  5.1 0.9 convert_multiply_fusion
  5.9 16.0 %window0.1 = bf16[6,227,512]{2,1,0:T(8,128)(2,1)} custom-call(bf16[227,512]{1,0:T(8,128)(2,1)} %x_ref.1), custom_call_target="tpu_custom_call" | custom-call | tf_op jit(solution)/shard_map/window0/pallas_call | solution.py:180
  21.9 7.2 %multiply_convert_fusion = (bf16[6,512,512]{2,1,0:T(8,128)(2,1)}, bf16[6,512,512]{2,1,0:T(8,128)(2,1)}, f32[6,512,512]{2,1,0:T(8,128)S(1)}) fusion(bf16[6,227,512]{2,1,0:T(8,128)(2,1)} %window0.1, bf16[227,512]{1,0:T(8,128)(2,1)} %refs_6_.1), kind=kOutput, calls=%fused_computation.6 | convolution fusion | flops 729808896 | bytes 14210048 | tf_op jit(solution)/shard_map/dot_general | solution.py:612
  29.1 0.0 copy-start.3
  29.1 1.7 %fusion.3 = bf16[3072,512]{1,0:T(8,128)(2,1)S(1)} fusion(f32[6,512,512]{2,1,0:T(8,128)S(1)} %get-tuple-element.29), kind=kLoop, calls=%fused_computation.9 | loop fusion | flops 7864320 | bytes 9437184 | tf_op jit(solution)/shard_map/convert_element_type | solution.py:615
  30.8 0.0 copy-done.3
  30.8 3.5 %convolution_convert_fusion = bf16[3072,512]{1,0:T(8,128)(2,1)} fusion(bf16[3072,512]{1,0:T(8,128)(2,1)S(1)} %fusion.3, bf16[512,512]{1,0:T(8,128)(2,1)S(1)} %copy-done.3), kind=kOutput, calls=%fused_computation.10 | convolution fusion | flops 1612185600 | bytes 6815744 | tf_op jit(solution)/shard_map/dot_general | solution.py:616
  34.3 10.6 %gather_fusion = bf16[2560,512]{1,0:T(8,128)(2,1)} fusion(bf16[3072,512]{1,0:T(8,128)(2,1)} %convolution_convert_fusion, s32[3072]{0:T(1024)S(1)} %pad_clamp_fusion), kind=kCustom, calls=%fused_computation | custom fusion | bytes 5253120 | tf_op jit(solution)/shard_map/gather | solution.py:619
  45.0 0.0 copy-start.1
  45.0 6.7 %encode.1 = (bf16[2560,512]{1,0:T(8,128)(2,1)}, bf16[2560,512]{1,0:T(8,128)(2,1)}, bf16[2560,512]{1,0:T(8,128)(2,1)}, f32[2560,1]{1,0:T(8,128)}, bf16[64,512]{1,0:T(8,128)(2,1)}) custom-call(bf16[2560,512]{1,0:T(8,128)(2,1)} %gather_fusion, f32[64,512]{1,0:T(8,128)} %fusion.15.d_ref, bf16[64,512]{1,0:T(8,128)(2,1)} %m_ref.1, bf16[512,512]{1,0:T(8,128)(2,1)} %w_ref.3), custom_call_target="tpu_custom_call" | custom-call | tf_op jit(solution)/shard_map/encode/pallas_call | solution.py:546
  51.7 0.0 copy-done
  51.7 1.7 %convolution_convert_fusion.3.x_ref = bf16[64,512]{1,0:T(8,128)(2,1)} fusion(bf16[64,512]{1,0:T(8,128)(2,1)} %get-tuple-element.14, bf16[512,512]{1,0:T(8,128)(2,1)S(1)} %copy-done), kind=kOutput, calls=%fused_computation.16 | convolution fusion | flops 33587200 | bytes 655360 | tf_op jit(solution)/shard_map/dot_general | solution.py:623
  53.3 0.0 copy-done.1
  53.4 1.0 fusion.16
  54.4 0.0 copy-start.2
  54.4 9.3 %window1.1 = bf16[6,64,512]{2,1,0:T(8,128)(2,1)} custom-call(bf16[64,512]{1,0:T(8,128)(2,1)} %convolution_convert_fusion.3.x_ref), custom_call_target="tpu_custom_call" | custom-call | tf_op jit(solution)/shard_map/window1/pallas_call | solution.py:180
  63.7 0.0 copy-start.5
  63.7 1.8 %fusion.13 = (bf16[64,512]{1,0:T(8,128)(2,1)S(1)}, f32[64,512]{1,0:T(8,128)S(1)}, bf16[6,64,512]{2,1,0:T(8,128)(2,1)S(1)}) fusion(f32[64,512]{1,0:T(8,128)S(1)} %convert_multiply_fusion, f32[64,512]{1,0:T(8,128)S(1)} %fusion.16, bf16[384,512,1]{1,0,2:T(8,128)(2,1)} %bitcast.54, s32[6,64]{1,0:T(8,128)S(1)} %subtract_bitcast_fusion), kind=kOutput, calls=%fused_computation.38 | convolution fusion | flops 153632768 | bytes 1246720 | tf_op jit(solution)/shard_map/dot_general | solution.py:628
  65.5 0.0 copy-done.2
  65.5 0.7 add_convert_fusion
  66.2 1.2 convolution_convert_fusion.2
  67.4 8.5 %return2.1 = f32[64,512]{1,0:T(8,128)} custom-call(bf16[6,64,512]{2,1,0:T(8,128)(2,1)} %bitcast.55), custom_call_target="tpu_custom_call" | custom-call | tf_op jit(solution)/shard_map/return2/pallas_call | solution.py:319
  75.9 0.0 copy-done.5
  75.9 1.2 convolution_add_fusion.2
  77.1 0.9 convolution_add_fusion.1.u_ref
  78.0 0.0 copy-start.6
  78.0 7.3 %decode.1 = (bf16[2560,512]{1,0:T(8,128)(2,1)}, bf16[2560,512]{1,0:T(8,128)(2,1)}) custom-call(f32[64,512]{1,0:T(8,128)} %convolution_add_fusion.1.u_ref, bf16[2560,512]{1,0:T(8,128)(2,1)} %get-tuple-element.16.n_ref, f32[2560,1]{1,0:T(8,128)} %get-tuple-element.17.i_ref, bf16[2560,512]{1,0:T(8,128)(2,1)} %get-tuple-element.18.l_ref, bf16[512,512]{1,0:T(8,128)(2,1)} %w_ref.3), custom_call_target="tpu_custom_call" | custom-call | tf_op jit(solution)/shard_map/decode/pallas_call | solution.py:580
  85.3 0.0 copy-done.6
  85.3 4.1 %convolution_convert_fusion.1 = bf16[512,512]{1,0:T(8,128)(2,1)} fusion(bf16[2560,512]{1,0:T(8,128)(2,1)S(1)} %copy-done.6, bf16[2560,512]{1,0:T(8,128)(2,1)} %get-tuple-element.19), kind=kOutput, calls=%fused_computation.11 | convolution fusion | flops 1342439424 | bytes 5767168 | tf_op jit(solution)/shard_map/dot_general | solution.py:27
  89.4 57.0 %tail.1 = (bf16[32,16,512]{2,1,0:T(8,128)(2,1)}, bf16[32,16,512]{2,1,0:T(8,128)(2,1)}, f32[227,512]{1,0:T(8,128)}) custom-call(bf16[32,16,512]{2,1,0:T(8,128)(2,1)} %bitcast.53, s32[1,2560]{1,0:T(1,128)} %broadcast_in_dim_reshape.4.refs_1_, bf16[2560,512]{1,0:T(8,128)(2,1)} %get-tuple-element.20.refs_2_, bf16[6,512,512]{2,1,0:T(8,128)(2,1)} %get-tuple-element.27.refs_3_, ...), custom_call_target="tpu_custom_call" | custom-call | tf_op jit(solution)/shard_map/tail/pallas_call | solution.py:501
  146.4 0.0 copy-start.4
  146.4 2.9 %bitcast_convert_fusion = (f32[512,512]{1,0:T(8,128)}, f32[512,512]{1,0:T(8,128)}) fusion(bf16[32,16,512]{2,1,0:T(8,128)(2,1)} %get-tuple-element.23, bf16[32,16,512]{2,1,0:T(8,128)(2,1)} %get-tuple-element.22), kind=kLoop, calls=%fused_computation.23 | loop fusion | flops 524288 | bytes 3145728 | tf_op jit(solution)/shard_map/convert_element_type | solution.py:653
  149.3 0.0 copy-done.4
  149.3 0.8 copy.19
  (2 shorter events, 0.0 us)
Async XLA Ops:
  0.6 51.0 %copy-start = (bf16[512,512]{1,0:T(8,128)(2,1)S(1)}, bf16[512,512]{1,0:T(8,128)(2,1)}, u32[]{:S(2)}) copy-start(bf16[512,512]{1,0:T(8,128)(2,1)} %param.17) | copy-start | bytes 1572868
  29.1 1.7 %copy-start.3 = (bf16[512,512]{1,0:T(8,128)(2,1)S(1)}, bf16[512,512]{1,0:T(8,128)(2,1)}, u32[]{:S(2)}) copy-start(bf16[512,512]{1,0:T(8,128)(2,1)} %refs_5_.1) | copy-start | bytes 1572868
  45.0 8.4 %copy-start.1 = (bf16[512,512]{1,0:T(8,128)(2,1)S(1)}, bf16[512,512]{1,0:T(8,128)(2,1)}, u32[]{:S(2)}) copy-start(bf16[512,512]{1,0:T(8,128)(2,1)} %param.18) | copy-start | bytes 1572868
  54.4 11.1 %copy-start.2 = (bf16[64,512]{1,0:T(8,128)(2,1)S(1)}, bf16[64,512]{1,0:T(8,128)(2,1)}, u32[]{:S(2)}) copy-start(bf16[64,512]{1,0:T(8,128)(2,1)} %get-tuple-element.14) | copy-start | bytes 196612
  63.7 12.2 %copy-start.5 = (bf16[64,512]{1,0:T(8,128)(2,1)S(1)}, bf16[64,512]{1,0:T(8,128)(2,1)}, u32[]{:S(2)}) copy-start(bf16[64,512]{1,0:T(8,128)(2,1)} %param.21) | copy-start | bytes 196612
  78.0 7.3 %copy-start.6 = (bf16[2560,512]{1,0:T(8,128)(2,1)S(1)}, bf16[2560,512]{1,0:T(8,128)(2,1)}, u32[]{:S(2)}) copy-start(bf16[2560,512]{1,0:T(8,128)(2,1)} %get-tuple-element.15) | copy-start | bytes 7864324
  146.4 2.9 %copy-start.4 = (f32[227,512]{1,0:T(8,128)S(1)}, f32[227,512]{1,0:T(8,128)}, u32[]{:S(2)}) copy-start(f32[227,512]{1,0:T(8,128)} %get-tuple-element.37) | copy-start | bytes 1394692

commit v5 on v3

--- a/solution.py
+++ b/solution.py
@@ -590,7 +590,7 @@
     projected = jnp.dot(hidden, w_src, preferred_element_type=F32).astype(BF16)
     dest_term = jnp.dot(mesh_in, w_dst, preferred_element_type=F32)
     grid_local = (g2m_src - (band_index * (nodes * subs) - nodes)).reshape(-1)
-    gathered = jnp.take(projected, grid_local, axis=0)
+    gathered = projected.at[grid_local].get(mode="promise_in_bounds")
     active, slope, normed, inverse, hidden_mesh = encode(
         gathered, dest_term, mesh_in, w_edge, enc_count, 16
     )

time: 150 us -> 148 us (0.987)
  other arithmetic: 10 us -> 7.6 us
    select_n x2 -> x1, other arithmetic: 2.47 us -> 0.04 us  [body(): gathered = projected.at[grid_local].get(mode='promise_in_bounds')]
where the time goes in v5:
time: 148 us; the launch traced here: 147 us
  Pallas kernels  86.4 us (58%)
  matrix products  38.1 us (26%)
  local copies, waits for them, and re-layouts  14.5 us (10%)
  other arithmetic  7.6 us (5%)
    pallas_call x1, Pallas kernels, tail(): pl.pallas_call(functools.partial(tail_kernel, bands, subs, len(values)),...  38.6 us
    pallas_call x2, Pallas kernels, fetch_window(): pl.pallas_call(functools.partial(window_kernel, bands, subs), out_shape=j...  25.3 us
    dot_general x4, matrix products, first_contract(): lax.dot_general(left, right, (((0,), (0,)), ((), ())), preferred_element_...  18.2 us
    gather x1, local copies, waits for them, and re-layouts, body(): gathered = projected.at[grid_local].get(mode='promise_in_bounds')  10.7 us
    pallas_call x1, Pallas kernels, return_window(): pl.pallas_call(functools.partial(return_kernel, bands, subs), out_shape=j...  8.47 us
    pallas_call x1, Pallas kernels, decode(): pl.pallas_call(functools.partial(decode_kernel, edges), grid=(rows // til...  7.3 us
    pallas_call x1, Pallas kernels, encode(): pl.pallas_call(functools.partial(encode_kernel, edges), grid=(rows // til...  6.78 us
    dot_general x3, matrix products, times_transpose(): lax.dot_general(left, right, (((1,), (1,)), ((), ())), preferred_element_...  5.38 us

profile of v5, /device:TPU:13, one launch (start us, length us, event | category | flops | bytes accessed | tf_op | source)
XLA Modules:
  0.0 147.5 jit_solution(11639898473997258200)
XLA Ops:
  0.6 0.0 copy-start
  0.7 0.7 subtract_bitcast_fusion
  1.4 0.1 eq.60
  1.5 0.7 broadcast_subtract_fusion
  2.2 0.1 copy.15
  2.3 0.1 reshape.95
  2.4 0.1 eq.56
  2.5 1.9 %fusion.24.d_ref = f32[64,512]{1,0:T(8,128)} fusion(bf16[64,512]{1,0:T(8,128)(2,1)} %m_ref.1, bf16[512,512]{1,0:T(8,128)(2,1)} %param.15), kind=kOutput, calls=%fused_computation.50 | convolution fusion | flops 33554432 | bytes 720896 | tf_op jit(solution)/shard_map/dot_general | solution.py:591
  4.5 0.9 convert_multiply_fusion
  5.3 16.0 %window0.1 = bf16[6,227,512]{2,1,0:T(8,128)(2,1)} custom-call(bf16[227,512]{1,0:T(8,128)(2,1)} %x_ref.1), custom_call_target="tpu_custom_call" | custom-call | tf_op jit(solution)/shard_map/window0/pallas_call | solution.py:180
  21.3 2.5 %fusion.17 = f32[6,512,512]{2,1,0:T(8,128)S(1)} fusion(bf16[6,227,512]{2,1,0:T(8,128)(2,1)} %window0.1, bf16[227,512]{1,0:T(8,128)(2,1)} %param.13), kind=kOutput, calls=%fused_computation.37 | convolution fusion | flops 714080256 | bytes 7918592 | tf_op jit(solution)/shard_map/dot_general | solution.py:586
  23.8 0.0 copy-start.1
  23.8 1.7 %fusion.5 = bf16[3072,512]{1,0:T(8,128)(2,1)S(1)} fusion(f32[6,512,512]{2,1,0:T(8,128)S(1)} %fusion.17), kind=kLoop, calls=%fused_computation.10 | loop fusion | flops 7864320 | bytes 9437184 | tf_op jit(solution)/shard_map/convert_element_type | solution.py:589
  25.5 0.9 copy-done.1
  26.5 1.7 %copy-done.2 = bf16[3072,512]{1,0:T(8,128)(2,1)} copy-done((bf16[3072,512]{1,0:T(8,128)(2,1)}, bf16[3072,512]{1,0:T(8,128)(2,1)S(1)}, u32[]{:S(2)}) %copy-start.2) | copy-done | bytes 3145752
  28.2 0.0 copy-done
  28.2 3.4 %convolution_convert_fusion = bf16[3072,512]{1,0:T(8,128)(2,1)} fusion(bf16[3072,512]{1,0:T(8,128)(2,1)S(1)} %fusion.5, bf16[512,512]{1,0:T(8,128)(2,1)S(1)} %copy-done), kind=kOutput, calls=%fused_computation.16 | convolution fusion | flops 1612185600 | bytes 6815744 | tf_op jit(solution)/shard_map/dot_general | solution.py:590
  31.6 10.7 %gather_fusion = bf16[2560,512]{1,0:T(8,128)(2,1)} fusion(bf16[3072,512]{1,0:T(8,128)(2,1)} %convolution_convert_fusion, s32[3072]{0:T(1024)S(1)} %pad_clamp_fusion), kind=kCustom, calls=%fused_computation | custom fusion | bytes 5253120 | tf_op jit(solution)/shard_map/gather | solution.py:593
  42.3 6.8 %encode.1 = (bf16[2560,512]{1,0:T(8,128)(2,1)}, bf16[2560,512]{1,0:T(8,128)(2,1)}, bf16[2560,512]{1,0:T(8,128)(2,1)}, f32[2560,1]{1,0:T(8,128)}, bf16[64,512]{1,0:T(8,128)(2,1)}) custom-call(bf16[2560,512]{1,0:T(8,128)(2,1)} %gather_fusion, f32[64,512]{1,0:T(8,128)} %fusion.24.d_ref, bf16[64,512]{1,0:T(8,128)(2,1)} %m_ref.1, bf16[512,512]{1,0:T(8,128)(2,1)} %w_ref.3), custom_call_target="tpu_custom_call" | custom-call | tf_op jit(solution)/shard_map/encode/pallas_call | solution.py:520
  49.0 0.0 copy-done.4
  49.1 1.7 %convolution_convert_fusion.5.x_ref = bf16[64,512]{1,0:T(8,128)(2,1)} fusion(bf16[64,512]{1,0:T(8,128)(2,1)} %get-tuple-element.14, bf16[512,512]{1,0:T(8,128)(2,1)S(1)} %copy-done.4), kind=kOutput, calls=%fused_computation.25 | convolution fusion | flops 33587200 | bytes 655360 | tf_op jit(solution)/shard_map/dot_general | solution.py:597
  50.7 0.0 copy-done.5
  50.7 1.0 fusion.25
  51.8 0.0 copy-start.7
  51.8 9.3 %window1.1 = bf16[6,64,512]{2,1,0:T(8,128)(2,1)} custom-call(bf16[64,512]{1,0:T(8,128)(2,1)} %convolution_convert_fusion.5.x_ref), custom_call_target="tpu_custom_call" | custom-call | tf_op jit(solution)/shard_map/window1/pallas_call | solution.py:180
  61.1 0.0 copy-start.9
  61.1 1.8 %fusion.22 = (bf16[64,512]{1,0:T(8,128)(2,1)S(1)}, f32[64,512]{1,0:T(8,128)S(1)}, bf16[6,64,512]{2,1,0:T(8,128)(2,1)S(1)}) fusion(f32[64,512]{1,0:T(8,128)S(1)} %convert_multiply_fusion, f32[64,512]{1,0:T(8,128)S(1)} %fusion.25, bf16[384,512,1]{1,0,2:T(8,128)(2,1)} %bitcast.79, s32[6,64]{1,0:T(8,128)S(1)} %subtract_bitcast_fusion), kind=kOutput, calls=%fused_computation.48 | convolution fusion | flops 153632768 | bytes 1246720 | tf_op jit(solution)/shard_map/dot_general | solution.py:602
  62.9 0.0 copy-done.7
  62.9 0.7 add_convert_fusion
  63.5 1.2 convolution_convert_fusion.4
  64.8 8.5 %return2.1 = f32[64,512]{1,0:T(8,128)} custom-call(bf16[6,64,512]{2,1,0:T(8,128)(2,1)} %bitcast.80), custom_call_target="tpu_custom_call" | custom-call | tf_op jit(solution)/shard_map/return2/pallas_call | solution.py:315
  73.3 0.0 copy-done.9
  73.3 1.2 convolution_add_fusion.2
  74.5 0.9 convolution_add_fusion.1.u_ref
  75.4 7.3 %decode.1 = (bf16[2560,512]{1,0:T(8,128)(2,1)}, bf16[2560,512]{1,0:T(8,128)(2,1)}) custom-call(f32[64,512]{1,0:T(8,128)} %convolution_add_fusion.1.u_ref, bf16[2560,512]{1,0:T(8,128)(2,1)} %get-tuple-element.15.n_ref, f32[2560,1]{1,0:T(8,128)} %get-tuple-element.16.i_ref, bf16[2560,512]{1,0:T(8,128)(2,1)} %get-tuple-element.17.l_ref, bf16[512,512]{1,0:T(8,128)(2,1)} %w_ref.3), custom_call_target="tpu_custom_call" | custom-call | tf_op jit(solution)/shard_map/decode/pallas_call | solution.py:554
  82.7 0.0 slice-start
  82.7 4.2 %convolution_convert_fusion.3 = bf16[512,512]{1,0:T(8,128)(2,1)} fusion(bf16[2560,512]{1,0:T(8,128)(2,1)S(1)} %copy-done.10, bf16[2560,512]{1,0:T(8,128)(2,1)} %get-tuple-element.20), kind=kOutput, calls=%fused_computation.20 | convolution fusion | flops 1342439424 | bytes 5767168 | tf_op jit(solution)/shard_map/dot_general | solution.py:27
  87.0 10.1 %fusion.10 = bf16[3072,512]{1,0:T(8,128)(2,1)S(1)} fusion(bf16[2560,512]{1,0:T(8,128)(2,1)S(1)} %copy-done.11, s32[2560]{0:T(1024)S(1)} %eq.56), kind=kOutput, calls=%fused_computation.15 | convolution fusion | flops 8062500864 | bytes 5777408 | tf_op jit(solution)/shard_map/dot_general | solution.py:27
  97.1 0.0 slice-done
  97.1 0.0 slice-done.1
  97.1 0.0 copy-start.3
  97.1 3.3 %fusion.9 = bf16[3072,512]{1,0:T(8,128)(2,1)S(1)} fusion(f32[6,512,512]{2,1,0:T(8,128)S(1)} %bitcast.75, bf16[3072,512]{1,0:T(8,128)(2,1)S(1)} %fusion.10, bf16[512,512]{1,0:T(8,128)(2,1)S(1)} %copy-done), kind=kOutput, calls=%fused_computation.14 | convolution fusion | flops 1624768512 | bytes 13107200 | tf_op jit(solution)/shard_map/dot_general | solution.py:23
  100.4 0.0 copy-start.6
  100.4 2.6 %convolution_convert_fusion.2 = bf16[512,512]{1,0:T(8,128)(2,1)} fusion(bf16[3072,512]{1,0:T(8,128)(2,1)S(1)} %copy-done.3, bf16[3072,512]{1,0:T(8,128)(2,1)S(1)} %fusion.10), kind=kOutput, calls=%fused_computation.19 | convolution fusion | flops 1610874880 | bytes 6815744 | tf_op jit(solution)/shard_map/dot_general | solution.py:27
  103.0 2.2 %fusion.11.refs_2_ = bf16[6,227,512]{2,1,0:T(8,128)(2,1)} fusion(bf16[6,512,512]{2,1,0:T(8,128)(2,1)S(1)} %bitcast.76, bf16[227,512]{1,0:T(8,128)(2,1)S(1)} %copy-done.6), kind=kOutput, calls=%fused_computation.18 | convolution fusion | flops 714777600 | bytes 4772864 | tf_op jit(solution)/shard_map/dot_general | solution.py:618
  105.2 38.6 %tail.1 = (bf16[32,16,512]{2,1,0:T(8,128)(2,1)}, bf16[32,16,512]{2,1,0:T(8,128)(2,1)}, f32[227,512]{1,0:T(8,128)}) custom-call(bf16[32,16,512]{2,1,0:T(8,128)(2,1)} %bitcast.78, bf16[32,16,512]{2,1,0:T(8,128)(2,1)} %bitcast.77, bf16[6,227,512]{2,1,0:T(8,128)(2,1)} %fusion.11.refs_2_), custom_call_target="tpu_custom_call" | custom-call | tf_op jit(solution)/shard_map/tail/pallas_call | solution.py:480
  143.8 2.9 %bitcast_convert_fusion = (f32[512,512]{1,0:T(8,128)}, f32[512,512]{1,0:T(8,128)}) fusion(bf16[32,16,512]{2,1,0:T(8,128)(2,1)} %get-tuple-element.23, bf16[32,16,512]{2,1,0:T(8,128)(2,1)} %get-tuple-element.22), kind=kLoop, calls=%fused_computation.32 | loop fusion | flops 524288 | bytes 3145728 | tf_op jit(solution)/shard_map/convert_element_type | solution.py:628
  146.7 0.8 copy.18
  (15 shorter events, 0.1 us)
Async XLA Ops:
  0.6 27.5 %copy-start = (bf16[512,512]{1,0:T(8,128)(2,1)S(1)}, bf16[512,512]{1,0:T(8,128)(2,1)}, u32[]{:S(2)}) copy-start(bf16[512,512]{1,0:T(8,128)(2,1)} %param.14) | copy-start | bytes 1572868
  23.8 2.7 %copy-start.1 = (f32[6,512,512]{2,1,0:T(8,128)}, f32[6,512,512]{2,1,0:T(8,128)S(1)}, u32[]{:S(2)}) copy-start(f32[6,512,512]{2,1,0:T(8,128)S(1)} %fusion.17) | copy-start | bytes 18874372
  26.5 1.7 %copy-start.2 = (bf16[3072,512]{1,0:T(8,128)(2,1)}, bf16[3072,512]{1,0:T(8,128)(2,1)S(1)}, u32[]{:S(2)}) copy-start(bf16[3072,512]{1,0:T(8,128)(2,1)S(1)} %fusion.5) | copy-start | bytes 9437188
  42.3 6.8 %copy-start.4 = (bf16[512,512]{1,0:T(8,128)(2,1)S(1)}, bf16[512,512]{1,0:T(8,128)(2,1)}, u32[]{:S(2)}) copy-start(bf16[512,512]{1,0:T(8,128)(2,1)} %param.17) | copy-start | bytes 1572868
  42.3 8.5 %copy-start.5 = (bf16[512,512]{1,0:T(8,128)(2,1)S(1)}, bf16[512,512]{1,0:T(8,128)(2,1)}, u32[]{:S(2)}) copy-start(bf16[512,512]{1,0:T(8,128)(2,1)} %param.18) | copy-start | bytes 1572868
  51.8 11.1 %copy-start.7 = (bf16[64,512]{1,0:T(8,128)(2,1)S(1)}, bf16[64,512]{1,0:T(8,128)(2,1)}, u32[]{:S(2)}) copy-start(bf16[64,512]{1,0:T(8,128)(2,1)} %get-tuple-element.14) | copy-start | bytes 196612
  61.1 12.2 %copy-start.9 = (bf16[64,512]{1,0:T(8,128)(2,1)S(1)}, bf16[64,512]{1,0:T(8,128)(2,1)}, u32[]{:S(2)}) copy-start(bf16[64,512]{1,0:T(8,128)(2,1)} %param.21) | copy-start | bytes 196612
  75.4 7.3 %copy-start.10 = (bf16[2560,512]{1,0:T(8,128)(2,1)S(1)}, bf16[2560,512]{1,0:T(8,128)(2,1)}, u32[]{:S(2)}) copy-start(bf16[2560,512]{1,0:T(8,128)(2,1)} %get-tuple-element.19) | copy-start | bytes 7864324
  82.7 4.3 %copy-start.11 = (bf16[2560,512]{1,0:T(8,128)(2,1)S(1)}, bf16[2560,512]{1,0:T(8,128)(2,1)}, u32[]{:S(2)}) copy-start(bf16[2560,512]{1,0:T(8,128)(2,1)} %get-tuple-element.18) | copy-start | bytes 7864324
  82.7 14.4 %slice-start = ((s8[6291456]{0:T(1024)(128)(4,1)}), s8[4194304]{0:T(1024)(128)(4,1)S(1)}, s32[]{:S(2)}) async-start(s8[6291456]{0:T(1024)(128)(4,1)} %bitcast.74), calls=%async_computation | async-start | bytes 8388608
  87.0 10.2 %slice-start.1 = ((s8[6291456]{0:T(1024)(128)(4,1)}), s8[2097152]{0:T(1024)(128)(4,1)S(1)}, s32[]{:S(2)}) async-start(s8[6291456]{0:T(1024)(128)(4,1)} %bitcast.74), calls=%async_computation.1 | async-start | bytes 4194304
  97.1 3.3 %copy-start.3 = (bf16[3072,512]{1,0:T(8,128)(2,1)S(1)}, bf16[3072,512]{1,0:T(8,128)(2,1)}, u32[]{:S(2)}) copy-start(bf16[3072,512]{1,0:T(8,128)(2,1)} %copy-done.2) | copy-start | bytes 9437188
  100.4 2.6 %copy-start.6 = (bf16[227,512]{1,0:T(8,128)(2,1)S(1)}, bf16[227,512]{1,0:T(8,128)(2,1)}, u32[]{:S(2)}) copy-start(bf16[227,512]{1,0:T(8,128)(2,1)} %param.13) | copy-start | bytes 697348
  143.8 2.9 %copy-start.8 = (f32[227,512]{1,0:T(8,128)S(1)}, f32[227,512]{1,0:T(8,128)}, u32[]{:S(2)}) copy-start(f32[227,512]{1,0:T(8,128)} %get-tuple-element.34) | copy-start | bytes 1394692
